TPU v7x, 128 devices: a whole 4x4x4 slice. The times are simulated.
128 devices in a mesh: ctx: 32 (over x, y, core), head: 4 (over z).
Axes of the slice: x: 4, y: 4, z: 4, core: 2. Of those that a mesh axis runs over, the one named last changes fastest.
Arguments:
- query: bfloat16 [32768, 4096], P('ctx', 'head'), may hold values from -150 to 150
- keys: bfloat16 [32768, 4096], P('ctx', 'head'), may hold values from -5.5 to 5.5, as said below
- values: bfloat16 [32768, 4096], P('ctx', 'head'), may hold values from -6 to 6
- lr_code: int32 [32768, 8], P('ctx', 'head'), may hold values from 2048 to 26623, as said below
- fast_weights: bfloat16 [8, 3, 512, 512], P('head'), may hold values from -0.25 to 0.25
- out_weight: bfloat16 [4096, 4096], P('head'), may hold values from -0.09375 to 0.09375
Outputs:
- layer_out: bfloat16 [32768, 4096], P('ctx', 'head')
- new_weights: bfloat16 [8, 3, 512, 512], P('head')
Inputs may be any that keep to these rules, and one draw needn't show every extreme that they name: `keys`: keys of order one. `lr_code`: Fixed-point learning-rate codes in units of 2**-14.
All inputs are finite; a program needn't handle non-finite values.
Results may differ from a plain program's by a relative error of at most 0.025.
Values may be sent and summed in bfloat16 or wider, within the bound.
A program may use at most 192 MiB of HBM per device.

v0:
```python
import math

import jax
import jax.numpy as jnp
from jax import lax
from jax.sharding import PartitionSpec as P

FW = 512
HEAD_DIM = 128
WINDOW = 256


base_rate = 0.05


def from_behind(block, axis, distance):
    devices = range(lax.axis_size(axis))
    route = [(i - distance, i) for i in devices if i - distance in devices]
    return lax.ppermute(block, axis, route)


def sent_to_all(value, axis):
    copies = jnp.broadcast_to(value, (lax.axis_size(axis), *value.shape))
    return lax.all_to_all(copies, axis, split_axis=0, concat_axis=0, tiled=True)


def of_everyone(value, axis):
    everything = sent_to_all(value, axis)
    return jnp.sum(everything, axis=0)


def attention(query, keys, values, rim_keys, rim_values, ctx_index):
    tok_rows, feat_width = query.shape
    head_count = feat_width // HEAD_DIM
    block_rows = min(512, tok_rows)
    q_all = query.reshape(tok_rows, head_count, HEAD_DIM)
    key_all = jnp.concatenate([rim_keys, keys], 0).reshape(tok_rows + WINDOW, head_count, HEAD_DIM)
    val_all = jnp.concatenate([rim_values, values], 0).reshape(
        tok_rows + WINDOW, head_count, HEAD_DIM
    )
    score_scale = 1.0 / math.sqrt(HEAD_DIM)
    shard_start = ctx_index * tok_rows

    def one_block(blk_index):
        row_start = blk_index * block_rows
        q_block = lax.dynamic_slice_in_dim(q_all, row_start, block_rows, 0)
        k_block = lax.dynamic_slice_in_dim(key_all, row_start, block_rows + WINDOW, 0)
        v_block = lax.dynamic_slice_in_dim(val_all, row_start, block_rows + WINDOW, 0)
        scores = (
            jnp.einsum("qhd,khd->hqk", q_block, k_block, preferred_element_type=jnp.float32)
            * score_scale
        )
        q_pos = shard_start + row_start + jnp.arange(block_rows, dtype=jnp.int32)[:, None]
        k_pos = (
            shard_start
            + row_start
            - WINDOW
            + jnp.arange(block_rows + WINDOW, dtype=jnp.int32)[None, :]
        )
        live = (k_pos <= q_pos) & (k_pos > q_pos - WINDOW) & (k_pos >= 0)
        scores = jnp.where(live[None], scores, jnp.float32(-1e30))
        top_score = jnp.max(scores, axis=-1, keepdims=True)
        exps = jnp.exp(scores - top_score)
        probs = (exps / jnp.sum(exps, axis=-1, keepdims=True)).astype(jnp.bfloat16)
        head_out = jnp.einsum("hqk,khd->qhd", probs, v_block, preferred_element_type=jnp.float32)
        return head_out.reshape(block_rows, feat_width)

    blocks_out = lax.map(one_block, jnp.arange(tok_rows // block_rows, dtype=jnp.int32))
    return blocks_out.reshape(tok_rows, feat_width)


def contract_rows(left, right):
    return lax.dot_general(
        left, right, (((0,), (0,)), ((), ())), preferred_element_type=jnp.float32
    )


def train_head(keys_h, values_h, rate_h, weights):
    gate_in = jnp.dot(keys_h, weights[0], preferred_element_type=jnp.float32)
    up_in = jnp.dot(keys_h, weights[1], preferred_element_type=jnp.float32)
    sigmoid_val = jax.nn.sigmoid(gate_in)
    gated_act = (gate_in * sigmoid_val * up_in).astype(jnp.bfloat16)
    pushed = (rate_h[:, None] * values_h.astype(jnp.float32)).astype(jnp.bfloat16)
    back_grad = lax.dot_general(
        pushed, weights[2], (((1,), (1,)), ((), ())), preferred_element_type=jnp.float32
    )
    d_gate = (back_grad * up_in * sigmoid_val * (1.0 + gate_in * (1.0 - sigmoid_val))).astype(
        jnp.bfloat16
    )
    d_up = (back_grad * gate_in * sigmoid_val).astype(jnp.bfloat16)
    return jnp.stack(
        [
            contract_rows(keys_h, d_gate),
            contract_rows(keys_h, d_up),
            contract_rows(gated_act, pushed),
        ]
    )


def renorm(start_w, grad_pull, step_size):
    base_w = start_w.astype(jnp.float32)
    updated = base_w + step_size[:, None, None, None] * grad_pull
    old_norm = jnp.sqrt(jnp.sum(base_w * base_w, axis=2, keepdims=True) + 1e-06)
    new_norm = jnp.sqrt(jnp.sum(updated * updated, axis=2, keepdims=True) + 1e-06)
    return (updated * (old_norm / new_norm)).astype(jnp.bfloat16)


def apply_head(query_h, weights):
    gate_in = jnp.dot(query_h, weights[0], preferred_element_type=jnp.float32)
    up_in = jnp.dot(query_h, weights[1], preferred_element_type=jnp.float32)
    gated_q = (gate_in * jax.nn.sigmoid(gate_in) * up_in).astype(jnp.bfloat16)
    head_out = jnp.dot(gated_q, weights[2], preferred_element_type=jnp.float32)
    return head_out * lax.rsqrt(jnp.mean(head_out * head_out, axis=-1, keepdims=True) + 1e-06)


def shards(query, keys, values, lr_code, fast_weights, out_weight):
    tok_rows = query.shape[0]
    contexts = lax.axis_size("ctx")
    ctx_index = lax.axis_index("ctx")
    tokens_all = tok_rows * contexts
    local_heads = fast_weights.shape[0]
    rim_keys, rim_values = from_behind(
        (keys[tok_rows - WINDOW :], values[tok_rows - WINDOW :]), "ctx", 1
    )
    rate = lr_code.astype(jnp.float32) * 2.0 ** (-14)
    rate_sum = of_everyone(jnp.sum(rate, axis=0), "ctx")
    step_size = base_rate / (math.sqrt(tokens_all) * (rate_sum / tokens_all))
    grad_pull = jnp.stack(
        [
            train_head(
                keys[:, head_idx * FW : (head_idx + 1) * FW],
                values[:, head_idx * FW : (head_idx + 1) * FW],
                rate[:, head_idx],
                fast_weights[head_idx],
            )
            for head_idx in range(local_heads)
        ]
    )
    attended = attention(query, keys, values, rim_keys, rim_values, ctx_index)
    pull_whole = lax.psum(grad_pull.astype(jnp.bfloat16), "ctx").astype(jnp.float32)
    new_weights = renorm(fast_weights, pull_whole, step_size)
    fast_out = jnp.concatenate(
        [
            apply_head(query[:, head_idx * FW : (head_idx + 1) * FW], new_weights[head_idx])
            for head_idx in range(local_heads)
        ],
        1,
    )
    merged = (attended + fast_out).astype(jnp.bfloat16)
    partial_out = jnp.dot(merged, out_weight, preferred_element_type=jnp.float32)
    layer_out = lax.psum_scatter(
        partial_out.astype(jnp.bfloat16), "head", scatter_dimension=1, tiled=True
    )
    return (layer_out, new_weights)


def solution(mesh):
    placed = (
        P("ctx", "head"),
        P("ctx", "head"),
        P("ctx", "head"),
        P("ctx", "head"),
        P("head", None, None, None),
        P("head", None),
    )
    return jax.shard_map(
        shards,
        mesh=mesh,
        in_specs=placed,
        out_specs=(P("ctx", "head"), P("head", None, None, None)),
        check_vma=False,
    )
```

profile of v0, /device:TPU:1, one launch (start us, length us, event | category | flops | bytes accessed | tf_op | source)
XLA Modules:
  0.0 341.1 jit_solution(2638874748239002762)
XLA Ops:
  9.1 4.7 %collective-permute-start = (bf16[256,1024]{1,0:T(8,128)(2,1)}, bf16[256,1024]{1,0:T(8,128)(2,1)}, u32[]{:S(2)}, u32[]{:S(2)}) collective-permute-start(bf16[256,1024]{1,0:T(8,128)(2,1)} %slice.94), channel_id=1, source_target_pairs={{0,4},{4,8},{8,12},{12,16},{16,20},{20,24},{24,28},{28,32},{32,36}... | collective-permute-start | bytes 1572872 | tf_op jit(solution)/shard_map/ppermute | solution.py:19
  13.8 4.0 %copy.46 = bf16[1024,1024]{0,1:T(8,128)(2,1)} copy(bf16[1024,1024]{1,0:T(8,128)(2,1)} %param.9) | data formatting | bytes 4194304 | tf_op args[1]
  38.0 7.4 %all-to-all-start = ((f32[32,1,2]{2,1,0:T(1,128)}), f32[32,1,2]{2,1,0:T(1,128)S(1)}, u32[]{:S(2)}, u32[]{:S(2)}) async-start(f32[32,1,2]{2,1,0:T(1,128)} %broadcast_in_dim.46), calls=%async_computation | async-start | bytes 32768 | tf_op jit(solution)/shard_map/all_to_all | solution.py:24
  45.6 2.8 copy.51
  48.5 4.1 %copy.45 = bf16[1024,1024]{0,1:T(8,128)(2,1)} copy(bf16[1024,1024]{1,0:T(8,128)(2,1)} %param.8) | data formatting | bytes 4194304 | tf_op args[0]
  52.6 2.8 pad_maximum_fusion.1
  55.4 4.6 %copy.44 = bf16[1280,1024]{0,1:T(8,128)(2,1)} copy(bf16[1280,1024]{1,0:T(8,128)(2,1)} %pad_maximum_fusion.1) | data formatting | bytes 5242880 | tf_op jit(solution)/shard_map/concatenate | solution.py:38
  60.0 2.7 pad_maximum_fusion.2
  62.7 144.2 %while.13 = (s32[]{:T(128)}, f32[2,512,1024]{1,0,2:T(2,128)}, s32[2]{0:T(128)S(1)}, bf16[1280,8,128]{0,2,1:T(8,128)(2,1)}, s32[]{:T(128)}, /*index=5*/bf16[1024,...) while((s32[]{:T(128)}, f32[2,512,1024]{1,0,2:T(2,128)}, ...), condition=%wide.region_3.4_spmd, body=%wide.region_0.3_spmd.sunk | while | flops 1637355520 | bytes 76332832 | solution.py:68
  64.0 8.1 %fusion.95 = f32[8,512,768]{2,1,0:T(8,128)} fusion(bf16[1280,8,128]{0,2,1:T(8,128)(2,1)} %get-tuple-element.254, s32[]{:T(128)S(6)} %select_n.37, bf16[1024,8,128]{0,2,1:T(8,128)(2,1)} %get-tuple-element.253, s32[]{:T(128)S(6)} %select_n.38), kind=kOutput, calls=%fused_computation.9.clone.1 | convolution fusion | flops 805306368 | bytes 15204360 | tf_op jit(solution)/shard_map/while/body/eval_jaxpr/qhd,khd->hqk/dot_general | solution.py:50
  72.6 16.3 %fusion.96 = (f32[8,512]{1,0:T(8,128)S(1)}, f32[8,512,768]{2,1,0:T(8,128)}) fusion(f32[8,512,768]{2,1,0:T(8,128)} %fusion.95, pred[512,768]{1,0:T(8,128)(4,1)S(1)} %and_and_fusion.2), kind=kOutput, calls=%fused_computation.132.clone.1 | output fusion | flops 18875136 | bytes 25575424 | tf_op jit(solution)/shard_map/while/body/eval_jaxpr/sub | solution.py:63
  88.9 5.9 %fusion.97 = f32[8,128,512]{2,1,0:T(8,128)S(1)} fusion(f32[8,512,768]{2,1,0:T(8,128)} %get-tuple-element.220, f32[8,512]{1,0:T(8,128)S(1)} %get-tuple-element.221, bf16[1280,8,128]{0,2,1:T(8,128)(2,1)S(1)} %copy-done.12, s32[]{:T(128)S(6)} %select_n.37), kind=kOutput, calls=%fused_computation.7.clone.1 | convolution fusion | flops 811597824 | bytes 16269316 | tf_op jit(solution)/shard_map/while/body/eval_jaxpr/hqk,khd->qhd/dot_general | solution.py:65
  97.0 37.9 %dynamic_update_slice.9 = f32[2,512,1024]{1,0,2:T(2,128)} dynamic-update-slice(f32[2,512,1024]{1,0,2:T(2,128)} %get-tuple-element.236, f32[1,512,1024]{1,0,2:T(1,128)S(1)} %copy.79, s32[]{:T(128)S(6)} %copy.83, s32[]{:T(128)} %constant.91.clone.1..sunk, s32[]{:T(128)} %constant.91.clone.1..sunk) | dynamic-update-slice | bytes 4194308 | tf_op jit(solution)/shard_map/while/body/jit(dynamic_update_index_in_dim)/dynamic_update_slice | solution.py:68
  136.1 8.2 %fusion.95 = f32[8,512,768]{2,1,0:T(8,128)} fusion(bf16[1280,8,128]{0,2,1:T(8,128)(2,1)} %get-tuple-element.254, s32[]{:T(128)S(6)} %select_n.37, bf16[1024,8,128]{0,2,1:T(8,128)(2,1)} %get-tuple-element.253, s32[]{:T(128)S(6)} %select_n.38), kind=kOutput, calls=%fused_computation.9.clone.1 | convolution fusion | flops 805306368 | bytes 15204360 | tf_op jit(solution)/shard_map/while/body/eval_jaxpr/qhd,khd->hqk/dot_general | solution.py:50
  144.7 16.3 %fusion.96 = (f32[8,512]{1,0:T(8,128)S(1)}, f32[8,512,768]{2,1,0:T(8,128)}) fusion(f32[8,512,768]{2,1,0:T(8,128)} %fusion.95, pred[512,768]{1,0:T(8,128)(4,1)S(1)} %and_and_fusion.2), kind=kOutput, calls=%fused_computation.132.clone.1 | output fusion | flops 18875136 | bytes 25575424 | tf_op jit(solution)/shard_map/while/body/eval_jaxpr/sub | solution.py:63
  161.0 5.9 %fusion.97 = f32[8,128,512]{2,1,0:T(8,128)S(1)} fusion(f32[8,512,768]{2,1,0:T(8,128)} %get-tuple-element.220, f32[8,512]{1,0:T(8,128)S(1)} %get-tuple-element.221, bf16[1280,8,128]{0,2,1:T(8,128)(2,1)S(1)} %copy-done.12, s32[]{:T(128)S(6)} %select_n.37), kind=kOutput, calls=%fused_computation.7.clone.1 | convolution fusion | flops 811597824 | bytes 16269316 | tf_op jit(solution)/shard_map/while/body/eval_jaxpr/hqk,khd->qhd/dot_general | solution.py:65
  169.1 37.9 %dynamic_update_slice.9 = f32[2,512,1024]{1,0,2:T(2,128)} dynamic-update-slice(f32[2,512,1024]{1,0,2:T(2,128)} %get-tuple-element.236, f32[1,512,1024]{1,0,2:T(1,128)S(1)} %copy.79, s32[]{:T(128)S(6)} %copy.83, s32[]{:T(128)} %constant.91.clone.1..sunk, s32[]{:T(128)} %constant.91.clone.1..sunk) | dynamic-update-slice | bytes 4194308 | tf_op jit(solution)/shard_map/while/body/jit(dynamic_update_index_in_dim)/dynamic_update_slice | solution.py:68
  206.9 5.3 %copy.77 = f32[128,8,2,512]{3,1,2,0:T(8,128)} copy(f32[128,8,2,512]{3,2,1,0:T(2,128)} %bitcast.139) | data formatting | bytes 8388608
  212.2 3.8 %fusion.14 = (f32[2,3,512]{2,1,0:T(4,128)S(1)}, f32[2,3,512]{2,1,0:T(4,128)S(1)}) fusion(bf16[2,3,512,512]{2,3,1,0:T(8,128)(2,1)S(1)} %copy-done, bf16[2,3,512,512]{2,3,1,0:T(8,128)(2,1)} %all-reduce.2.cloned.1.call-done, f32[2]{0:T(128)S(1)} %multiply_divide_fusion), kind=kLoop, calls=%fused_computation.25 | loop fusion | flops 12576768 | bytes 6316040 | tf_op jit(solution)/shard_map/reduce_sum | solution.py:103
  222.1 5.1 %multiply_reduce_fusion.1 = (f32[1024]{0:T(1024)S(1)}, f32[1024,512]{0,1:T(8,128)}) fusion(bf16[2,3,512,512]{2,3,1,0:T(8,128)(2,1)} %copy-done.2, f32[512,1024]{0,1:T(8,128)} %fusion.37, bf16[1024,1024]{1,0:T(8,128)(2,1)} %param.8), kind=kOutput, calls=%fused_computation.47 | convolution fusion | flops 1077935104 | bytes 6295552 | tf_op jit(solution)/shard_map/dot_general | solution.py:112
  227.2 4.7 %multiply_reduce_fusion.2 = (f32[1024]{0:T(1024)S(1)}, f32[1024,512]{0,1:T(8,128)}) fusion(bf16[2,3,512,512]{2,3,1,0:T(8,128)(2,1)S(1)} %copy-done.3, f32[512,1024]{0,1:T(8,128)} %fusion.41, bf16[1024,1024]{1,0:T(8,128)(2,1)} %param.8), kind=kOutput, calls=%fused_computation.48 | convolution fusion | flops 1077935104 | bytes 6295552 | tf_op jit(solution)/shard_map/dot_general | solution.py:112
  236.3 15.0 %convolution_convert_fusion = bf16[1024,4096]{1,0:T(8,128)(2,1)} fusion(bf16[1024,4096]{1,0:T(8,128)(2,1)} %param.13, f32[1024,1024]{0,1:T(8,128)S(1)} %bitcast.140, f32[1024,512]{0,1:T(8,128)S(1)} %broadcast_multiply_fusion, f32[1024,512]{0,1:T(8,128)S(1)} %broadcast_multiply_fusion.1), kind=kOutput, calls=%fused_computation.24 | convolution fusion | flops 8597274624 | bytes 25165824 | tf_op jit(solution)/shard_map/dot_general | solution.py:150
  251.3 2.8 copy.59
  254.1 80.2 %reduce-scatter.2.cloned.1.call-done = bf16[1024,1024]{1,0:T(8,128)(2,1)} async-done(((bf16[1024,4096]{1,0:T(8,128)(2,1)}), bf16[1024,1024]{1,0:T(8,128)(2,1)}) %reduce-scatter.2.cloned.1.call-update) | async-done | bytes 2097168 | tf_op jit(solution)/shard_map/reduce_scatter | solution.py:151
  (84 shorter events, 39.1 us)
Async XLA Ops:
  7.2 205.1 %all-reduce.2.cloned.1.call-start = ((), (), s32[]{:S(2)}) async-start(), calls=%async_computation.2 | async-start | bytes 6291456 | tf_op jit(solution)/shard_map/psum | solution.py:140
  9.1 12.8 %copy-start.1 = (bf16[1024,1024]{1,0:T(8,128)(2,1)S(1)}, bf16[1024,1024]{1,0:T(8,128)(2,1)}, u32[]{:S(2)}) copy-start(bf16[1024,1024]{1,0:T(8,128)(2,1)} %param.9) | copy-start | bytes 6291460
  9.1 43.5 %collective-permute-start = (bf16[256,1024]{1,0:T(8,128)(2,1)}, bf16[256,1024]{1,0:T(8,128)(2,1)}, u32[]{:S(2)}, u32[]{:S(2)}) collective-permute-start(bf16[256,1024]{1,0:T(8,128)(2,1)} %slice.94), channel_id=1, source_target_pairs={{0,4},{4,8},{8,12},{12,16},{16,20},{20,24},{24,28},{28,32},{32,36}... | collective-permute-start | bytes 1572872 | tf_op jit(solution)/shard_map/ppermute | solution.py:19
  19.7 3.9 %copy-start.6 = (bf16[2,3,512,512]{3,2,1,0:T(8,128)(2,1)S(1)}, bf16[2,3,512,512]{3,2,1,0:T(8,128)(2,1)}, u32[]{:S(2)}) copy-start(bf16[2,3,512,512]{3,2,1,0:T(8,128)(2,1)} %param.12) | copy-start | bytes 9437188
  19.7 40.3 %collective-permute-start.1 = (bf16[256,1024]{0,1:T(8,128)(2,1)}, bf16[256,1024]{0,1:T(8,128)(2,1)}, u32[]{:S(2)}, u32[]{:S(2)}) collective-permute-start(bf16[256,1024]{0,1:T(8,128)(2,1)} %slice.116), channel_id=1, source_target_pairs={{0,4},{4,8},{8,12},{12,16},{16,20},{20,24},{24,28},{28,32},{32,36}... | collective-permute-start | bytes 1572872 | tf_op jit(solution)/shard_map/ppermute | solution.py:19
  23.6 0.7 copy-start.14
  23.6 1.6 copy-start.10
  37.3 8.3 %copy-start.7 = (bf16[2,3,512,512]{3,2,1,0:T(8,128)(2,1)S(1)}, bf16[2,3,512,512]{3,2,1,0:T(8,128)(2,1)}, u32[]{:S(2)}) copy-start(bf16[2,3,512,512]{3,2,1,0:T(8,128)(2,1)} %param.12) | copy-start | bytes 9437188
  38.0 14.6 %all-to-all-start = ((f32[32,1,2]{2,1,0:T(1,128)}), f32[32,1,2]{2,1,0:T(1,128)S(1)}, u32[]{:S(2)}, u32[]{:S(2)}) async-start(f32[32,1,2]{2,1,0:T(1,128)} %broadcast_in_dim.46), calls=%async_computation | async-start | bytes 32768 | tf_op jit(solution)/shard_map/all_to_all | solution.py:24
  45.4 288.9 %reduce-scatter.2.cloned.1.call-start = ((), (), s32[]{:S(2)}) async-start(), calls=%async_computation.3 | async-start | bytes 10485760 | tf_op jit(solution)/shard_map/reduce_scatter | solution.py:151
  48.5 4.2 %copy-start.11 = (bf16[1024,1024]{1,0:T(8,128)(2,1)S(1)}, bf16[1024,1024]{1,0:T(8,128)(2,1)}, u32[]{:S(2)}) copy-start(bf16[1024,1024]{1,0:T(8,128)(2,1)} %param.10) | copy-start | bytes 6291460
  55.4 4.6 %copy-start.5 = (bf16[1024,1024]{0,1:T(8,128)(2,1)S(1)}, bf16[1024,1024]{0,1:T(8,128)(2,1)}, u32[]{:S(2)}) copy-start(bf16[1024,1024]{0,1:T(8,128)(2,1)} %copy.46) | copy-start | bytes 6291460
  72.5 16.3 %copy-start.12 = (bf16[1280,8,128]{0,2,1:T(8,128)(2,1)S(1)}, bf16[1280,8,128]{0,2,1:T(8,128)(2,1)}, u32[]{:S(2)}) copy-start(bf16[1280,8,128]{0,2,1:T(8,128)(2,1)} %get-tuple-element.251) | copy-start | bytes 7864324 | tf_op jit(solution)/shard_map/while
  144.7 16.3 %copy-start.12 = (bf16[1280,8,128]{0,2,1:T(8,128)(2,1)S(1)}, bf16[1280,8,128]{0,2,1:T(8,128)(2,1)}, u32[]{:S(2)}) copy-start(bf16[1280,8,128]{0,2,1:T(8,128)(2,1)} %get-tuple-element.251) | copy-start | bytes 7864324 | tf_op jit(solution)/shard_map/while
  206.9 5.3 %copy-start = (bf16[2,3,512,512]{2,3,1,0:T(8,128)(2,1)S(1)}, bf16[2,3,512,512]{2,3,1,0:T(8,128)(2,1)}, u32[]{:S(2)}) copy-start(bf16[2,3,512,512]{2,3,1,0:T(8,128)(2,1)} %copy.51) | copy-start | bytes 9437188
  212.2 3.8 %copy-start.4 = (bf16[2,3,512,512]{2,3,1,0:T(8,128)(2,1)S(1)}, bf16[2,3,512,512]{2,3,1,0:T(8,128)(2,1)}, u32[]{:S(2)}) copy-start(bf16[2,3,512,512]{2,3,1,0:T(8,128)(2,1)} %all-reduce.2.cloned.1.call-done) | copy-start | bytes 9437188
  216.0 1.6 copy-start.8
  217.6 2.4 copy-start.2
  222.1 5.1 %copy-start.3 = (bf16[2,3,512,512]{2,3,1,0:T(8,128)(2,1)S(1)}, bf16[2,3,512,512]{2,3,1,0:T(8,128)(2,1)}, u32[]{:S(2)}) copy-start(bf16[2,3,512,512]{2,3,1,0:T(8,128)(2,1)} %copy-done.2) | copy-start | bytes 9437188
  231.9 2.2 copy-start.13
  234.1 2.2 copy-start.9
Sparse Core Ops, SparseCore 0:
  37.5 111.2 all-reduce.1
  251.4 82.8 reduce-scatter.1
where the time goes:
time: 347 us; the launch traced here: 341 us
  local copies, waits for them, and re-layouts  112 us (32%)
  waiting for transfers between devices  80.2 us (23%)
  matrix products  69.5 us (20%)
  other arithmetic  48.9 us (14%)
  starting transfers between devices  14.6 us (4%)
  between operations  14.3 us (4%)
    reduce_scatter x1, waiting for transfers between devices, shards(): lax.psum_scatter(partial_out.astype(jnp.bfloat16), 'head', scatter_dimens...  80.2 us
    dynamic_update_slice x4, local copies, waits for them, and re-layouts, attention(): lax.map(one_block, jnp.arange(tok_rows // block_rows, dtype=jnp.int32))  80 us
    sub x2, other arithmetic, one_block(): exps = jnp.exp(scores - top_score)  32.6 us
    unnamed x33, local copies, waits for them, and re-layouts  22.1 us
    dot_general x2, matrix products, one_block(): jnp.einsum('qhd,khd->hqk', q_block, k_block, preferred_element_type=jnp.f...  16.3 us
    dot_general x1, matrix products, shards(): jnp.dot(merged, out_weight, preferred_element_type=jnp.float32)  15 us
    dot_general x2, matrix products, one_block(): jnp.einsum('hqk,khd->qhd', probs, v_block, preferred_element_type=jnp.flo...  11.8 us
    dot_general x2, matrix products, apply_head(): head_out = jnp.dot(gated_q, weights[2], preferred_element_type=jnp.float32)  9.8 us
  transfers between devices with their start and end apart: 5, of which 1 were waited for; matrix products, arithmetic and copies ran while one was open for 55% of the time, Pallas kernels for 0%

commit v1 on v0

v1 whole, which is shorter than its diff:
```python
import math

import jax
import jax.numpy as jnp
from jax import lax
from jax.experimental import pallas as pl
from jax.experimental.pallas import tpu as pltpu
from jax.sharding import PartitionSpec as P

FW = 512
HEAD_DIM = 128
WINDOW = 256
BASE_RATE = 0.05
BLOCK = 256
F32 = jnp.float32
BF16 = jnp.bfloat16
MESH = pl.DeviceIdType.MESH
MIB = 1024 * 1024


def dot(left, right, left_dim=1, right_dim=0):
    return lax.dot_general(
        left, right, (((left_dim,), (right_dim,)), ((), ())), preferred_element_type=F32
    )


def sigmoid(x):
    return 0.5 * jnp.tanh(0.5 * x) + 0.5


RIM_K, RIM_V, CORE_G, CORE_R = 0, 1, 2, 3
X_A, X_B, X_R = 3, 6, 9
Y_A, Y_B, Y_R = 12, 15, 18
GY_A, GY_B, GX_A, GX_B = 21, 24, 27, 30
CORE_P = 34
COPIES = 35
RING = 4


def update_kernel(
    q_hbm, k_hbm, v_hbm, code_ref, fw_hbm,
    att_ref, pull_hbm, rate_ref,
    q_buf, k_buf, v_buf, fw_buf, d_buf, gated_buf, pushed_buf,
    grad_out, grad_in, grad_sum, in_xa, in_xb, sum_a, sum_b, in_ya, in_yb,
    pull_buf, rate_out, rate_in, load_sem, store_sem, send_sem, recv_sem,
):
    ctx = lax.axis_index("ctx")
    core = lax.rem(ctx, 2)
    chip = lax.div(ctx, 2)
    y = lax.rem(chip, RING)
    x = lax.div(chip, RING)
    contexts = lax.axis_size("ctx")
    rows = k_hbm.shape[0]
    blocks = rows // BLOCK
    part = in_xa.shape[1]
    piece = in_ya.shape[1]
    half = grad_sum.shape[0] // 2

    def at(xx, yy, cc):
        return (xx * RING + yy) * 2 + cc

    partner = at(x, y, 1 - core)
    follower = lax.rem(ctx + 1, contexts)
    leader = lax.rem(ctx + contexts - 1, contexts)
    x_peer = [None] + [at(lax.rem(x + d, RING), y, core) for d in range(1, RING)]
    y_peer = [None] + [at(x, lax.rem(y + d, RING), core) for d in range(1, RING)]

    def load(src, dst, index):
        return pltpu.make_async_copy(src, dst, load_sem.at[index])

    first, second = 1 - core, core

    def lanes(head):
        return pl.ds(pl.multiple_of(head * FW, FW), FW)

    loads = {}
    for order, head in enumerate((first, second)):
        loads["w", order] = load(fw_hbm.at[head], fw_buf.at[head], 4 * order)
        loads["k", order] = load(
            k_hbm.at[:, lanes(head)], k_buf.at[head, pl.ds(WINDOW, rows)], 4 * order + 1
        )
        loads["v", order] = load(
            v_hbm.at[:, lanes(head)], v_buf.at[head, pl.ds(WINDOW, rows)], 4 * order + 2
        )
        loads["q", order] = load(q_hbm.at[:, lanes(head)], q_buf.at[head], 4 * order + 3)
    for name in ("w", "k", "v"):
        for order in range(2):
            loads[name, order].start()

    barrier = pltpu.get_barrier_semaphore()
    peers = [follower, leader] + x_peer[1:] + y_peer[1:]
    for peer in peers:
        pl.semaphore_signal(barrier, inc=1, device_id={"ctx": peer}, device_id_type=MESH)
    pl.semaphore_wait(barrier, len(peers))

    def remote(src, dst, index, peer):
        return pltpu.make_async_remote_copy(
            src_ref=src, dst_ref=dst, send_sem=send_sem.at[index], recv_sem=recv_sem.at[index],
            device_id={"ctx": peer}, device_id_type=MESH,
        )

    sent = []

    def send(copy):
        copy.start()
        sent.append(copy)
        return copy

    for order in range(2):
        loads["k", order].wait()
        loads["v", order].wait()
    for order in range(2):
        loads["q", order].start()
    rim = [
        send(remote(k_buf.at[:, pl.ds(rows, WINDOW)], k_buf.at[:, pl.ds(0, WINDOW)], RIM_K, follower)),
        send(remote(v_buf.at[:, pl.ds(rows, WINDOW)], v_buf.at[:, pl.ds(0, WINDOW)], RIM_V, follower)),
    ]

    rate = code_ref[...].astype(F32) * 2.0 ** (-14)
    rate_out[0] = jnp.broadcast_to(jnp.sum(rate, axis=1, keepdims=True), rate_out.shape[1:])
    core_rate = send(remote(rate_out.at[0], rate_in.at[0], CORE_R, partner))

    def train(head):
        def tokens(t, carry):
            start = pl.multiple_of(t * BLOCK, BLOCK)
            k_rows = k_buf[head, pl.ds(start + WINDOW, BLOCK)]
            v_rows = v_buf[head, pl.ds(start + WINDOW, BLOCK)].astype(F32)
            code_row = code_ref[pl.ds(head, 1), pl.ds(start, BLOCK)].astype(F32) * 2.0 ** (-14)
            column = jnp.transpose(jnp.broadcast_to(code_row, (8, BLOCK)))[:, 0:1]
            pushed = (column * v_rows).astype(BF16)
            gate_in = dot(k_rows, fw_buf[head, 0])
            up_in = dot(k_rows, fw_buf[head, 1])
            back = dot(pushed, fw_buf[head, 2], 1, 1)
            s = sigmoid(gate_in)
            gs = gate_in * s
            here = pl.ds(start, BLOCK)
            pushed_buf[here] = pushed
            gated_buf[here] = (gs * up_in).astype(BF16)
            d_buf[here, 0:FW] = (back * up_in * (s * (1.0 + gate_in * (1.0 - s)))).astype(BF16)
            d_buf[here, FW : 2 * FW] = (back * gs).astype(BF16)
            return carry

        lax.fori_loop(0, blocks, tokens, 0)

    def pulls(head, put):
        for i in range(FW // BLOCK):
            cols = pl.ds(i * BLOCK, BLOCK)
            k_cols = k_buf[head, pl.ds(WINDOW, rows), cols]
            both = dot(k_cols, d_buf[...], 0, 0)
            put(pl.ds(i * BLOCK, BLOCK), both[:, 0:FW])
            put(pl.ds(FW + i * BLOCK, BLOCK), both[:, FW : 2 * FW])
            put(pl.ds(2 * FW + i * BLOCK, BLOCK), dot(gated_buf[:, cols], pushed_buf[...], 0, 0))

    def put_out(where, value):
        grad_out[where] = value.astype(BF16)

    def put_sum(where, value):
        grad_sum[where] = (value + grad_in[where].astype(F32)).astype(BF16)

    loads["w", 0].wait()
    train(first)
    pulls(first, put_out)
    core_grad = send(remote(grad_out, grad_in, CORE_G, partner))
    loads["w", 1].wait()
    train(second)
    core_rate.wait_recv()
    rate_out[1] = rate_out[0] + rate_in[0]
    core_grad.wait_recv()
    pulls(second, put_sum)

    def aligned(start, size):
        return pl.ds(pl.multiple_of(start, 16), size)

    def ring_to(index):
        return lax.rem(index, RING)

    out_x = []
    for d in range(1, RING):
        out_x.append(send(remote(
            grad_sum.at[aligned(ring_to(x + d) * part, part)], in_xa.at[d - 1], X_A + d, x_peer[d])))
        out_x.append(send(remote(
            grad_sum.at[aligned(half + ring_to(y + d) * part, part)], in_xb.at[d - 1], X_B + d, y_peer[d])))
        out_x.append(send(remote(rate_out.at[1], rate_in.at[d], X_R + d, x_peer[d])))

    for copy in rim:
        copy.wait_recv()
    for order in range(2):
        loads["q", order].wait()

    row_id = lax.broadcasted_iota(jnp.int32, (BLOCK, BLOCK), 0)
    col_id = lax.broadcasted_iota(jnp.int32, (BLOCK, BLOCK), 1)
    scale = math.log2(math.e) / math.sqrt(HEAD_DIM)

    def attend(unit, carry):
        head = lax.div(unit, blocks)
        block = lax.rem(unit, blocks)
        start = pl.multiple_of(block * BLOCK, BLOCK)
        unseen = jnp.where((ctx == 0) & (block == 0), -1e30, 0.0).astype(F32)
        causal = col_id <= row_id
        for j in range(FW // HEAD_DIM):
            cols = pl.ds(j * HEAD_DIM, HEAD_DIM)
            q_rows = q_buf[head, pl.ds(start, BLOCK), cols]
            scores = dot(q_rows, k_buf[head, pl.ds(start, 2 * BLOCK), cols], 1, 1)
            live = jnp.where(causal, scores[:, BLOCK:], scores[:, :BLOCK] + unseen)
            top = jnp.max(live, axis=1, keepdims=True)
            exps = jnp.exp2((live - top) * scale)
            old = jnp.where(causal, 0.0, exps).astype(BF16)
            new = jnp.where(causal, exps, 0.0).astype(BF16)
            ones = jnp.ones((BLOCK, HEAD_DIM), BF16)
            v_old = jnp.concatenate([v_buf[head, pl.ds(start, BLOCK), cols], ones], 1)
            v_new = jnp.concatenate([v_buf[head, pl.ds(start + BLOCK, BLOCK), cols], ones], 1)
            both = dot(old, v_old) + dot(new, v_new)
            att_ref[head, pl.ds(start, BLOCK), cols] = (
                both[:, :HEAD_DIM] / both[:, HEAD_DIM:]
            ).astype(BF16)
        return carry

    units = 2 * blocks
    lax.fori_loop(0, units // 2, attend, 0)

    for copy in out_x:
        copy.wait_recv()

    def total(own, others):
        value = own.astype(F32)
        for i in range(RING - 1):
            value = value + others[i].astype(F32)
        return value

    sum_a[...] = total(grad_sum[aligned(x * part, part)], in_xa).astype(BF16)
    sum_b[...] = total(grad_sum[aligned(half + y * part, part)], in_xb).astype(BF16)
    rate_out[2] = rate_out[1] + rate_in[1] + rate_in[2] + rate_in[3]

    out_y = []
    for d in range(1, RING):
        out_y.append(send(remote(
            sum_a.at[aligned(ring_to(y + d) * piece, piece)], in_ya.at[d - 1], Y_A + d, y_peer[d])))
        out_y.append(send(remote(
            sum_b.at[aligned(ring_to(x + d) * piece, piece)], in_yb.at[d - 1], Y_B + d, x_peer[d])))
        out_y.append(send(remote(rate_out.at[2], rate_in.at[RING - 1 + d], Y_R + d, y_peer[d])))
    lax.fori_loop(units // 2, units // 2 + 1, attend, 0)
    for copy in out_y:
        copy.wait_recv()
    own_a = aligned(x * part + y * piece, piece)
    own_b = aligned(half + y * part + x * piece, piece)
    pull_buf[core, own_a] = total(sum_a[aligned(y * piece, piece)], in_ya).astype(BF16)
    pull_buf[core, own_b] = total(sum_b[aligned(x * piece, piece)], in_yb).astype(BF16)
    rate_ref[...] = rate_out[2] + rate_in[4] + rate_in[5] + rate_in[6]

    back_y = []
    for d in range(1, RING):
        mine_a, mine_b = pull_buf.at[core, own_a], pull_buf.at[core, own_b]
        back_y.append(send(remote(mine_a, mine_a, GY_A + d, y_peer[d])))
        back_y.append(send(remote(mine_b, mine_b, GY_B + d, x_peer[d])))
    lax.fori_loop(units // 2 + 1, units // 2 + 2, attend, 0)
    for copy in back_y:
        copy.wait_recv()

    back_x = []
    for d in range(1, RING):
        mine_a = pull_buf.at[core, aligned(x * part, part)]
        mine_b = pull_buf.at[core, aligned(half + y * part, part)]
        back_x.append(send(remote(mine_a, mine_a, GX_A + d, x_peer[d])))
        back_x.append(send(remote(mine_b, mine_b, GX_B + d, y_peer[d])))
    lax.fori_loop(units // 2 + 2, units, attend, 0)
    for copy in back_x:
        copy.wait_recv()

    across = send(remote(pull_buf.at[core], pull_buf.at[core], CORE_P, partner))
    store_own = pltpu.make_async_copy(pull_buf.at[core], pull_hbm.at[core], store_sem.at[0])
    store_own.start()
    across.wait_recv()
    store_other = pltpu.make_async_copy(pull_buf.at[1 - core], pull_hbm.at[1 - core], store_sem.at[1])
    store_other.start()
    for copy in sent:
        copy.wait_send()
    store_own.wait()
    store_other.wait()


def update(query, keys, values, code_t, fast_weights):
    rows, width = query.shape
    heads = width // FW
    pulled = 3 * FW
    part = pulled // 2 // RING
    piece = part // RING
    hbm = pl.BlockSpec(memory_space=pl.ANY)
    vmem = pl.BlockSpec(memory_space=pltpu.VMEM)
    return pl.pallas_call(
        update_kernel,
        out_shape=(
            jax.ShapeDtypeStruct((heads, rows, FW), BF16),
            jax.ShapeDtypeStruct((heads, pulled, FW), BF16),
            jax.ShapeDtypeStruct((heads, 128), F32),
        ),
        in_specs=[hbm, hbm, hbm, vmem, hbm],
        out_specs=(vmem, hbm, vmem),
        scratch_shapes=[
            pltpu.VMEM((heads, rows, FW), BF16),
            pltpu.VMEM((heads, rows + WINDOW, FW), BF16),
            pltpu.VMEM((heads, rows + WINDOW, FW), BF16),
            pltpu.VMEM((heads, 3, FW, FW), BF16),
            pltpu.VMEM((rows, 2 * FW), BF16),
            pltpu.VMEM((rows, FW), BF16),
            pltpu.VMEM((rows, FW), BF16),
            pltpu.VMEM((pulled, FW), BF16),
            pltpu.VMEM((pulled, FW), BF16),
            pltpu.VMEM((pulled, FW), BF16),
            pltpu.VMEM((RING - 1, part, FW), BF16),
            pltpu.VMEM((RING - 1, part, FW), BF16),
            pltpu.VMEM((part, FW), BF16),
            pltpu.VMEM((part, FW), BF16),
            pltpu.VMEM((RING - 1, piece, FW), BF16),
            pltpu.VMEM((RING - 1, piece, FW), BF16),
            pltpu.VMEM((heads, pulled, FW), BF16),
            pltpu.VMEM((3, heads, 128), F32),
            pltpu.VMEM((7, heads, 128), F32),
            pltpu.SemaphoreType.DMA((8,)),
            pltpu.SemaphoreType.DMA((2,)),
            pltpu.SemaphoreType.DMA((COPIES,)),
            pltpu.SemaphoreType.DMA((COPIES,)),
        ],
        compiler_params=pltpu.CompilerParams(
            collective_id=0, has_side_effects=True, vmem_limit_bytes=56 * MIB
        ),
        name="update",
    )(query, keys, values, code_t, fast_weights)


def renorm_kernel(tokens_all, rate_ref, pull_ref, fw_ref, new_ref):
    head = lax.div(pl.program_id(0), 3)
    rate_sum = jnp.where(head == 0, rate_ref[0:1, 0:1], rate_ref[1:2, 0:1])
    step = BASE_RATE / (math.sqrt(tokens_all) * (rate_sum / tokens_all))
    base = fw_ref[0].astype(F32)
    updated = base + step * pull_ref[0].astype(F32)
    old = jnp.sqrt(jnp.sum(base * base, axis=0, keepdims=True) + 1e-06)
    new = jnp.sqrt(jnp.sum(updated * updated, axis=0, keepdims=True) + 1e-06)
    new_ref[0] = (updated * (old / new)).astype(BF16)


def renorm(rate_sum, pull, fast_weights, tokens_all):
    count = pull.shape[0]
    matrix = pl.BlockSpec((1, FW, FW), lambda i: (i, 0, 0))

    def kernel(*refs):
        renorm_kernel(tokens_all, *refs)

    return pl.pallas_call(
        kernel,
        grid=(count,),
        out_shape=jax.ShapeDtypeStruct((count, FW, FW), BF16),
        in_specs=[pl.BlockSpec(rate_sum.shape, lambda i: (0, 0)), matrix, matrix],
        out_specs=matrix,
        name="renorm",
    )(rate_sum, pull, fast_weights)


SUBS = 4
HALF = 512


def project_kernel(
    q_hbm, att_hbm, nw_hbm, w_hbm, out_ref,
    q_buf, att_buf, nw_buf, w_buf, merged, out_buf, in_buf,
    load_sem, send_sem, recv_sem,
):
    me = lax.axis_index("head")
    n = lax.axis_size("head")
    ahead, behind = lax.rem(me + 1, n), lax.rem(me + n - 1, n)
    targets = (ahead, behind)
    rows = out_ref.shape[0]
    sub_rows = rows // SUBS
    heads = att_buf.shape[0]

    loads = []

    def load(src, dst):
        copy = pltpu.make_async_copy(src, dst, load_sem.at[len(loads)])
        copy.start()
        loads.append(copy)
        return copy

    nw_load = load(nw_hbm, nw_buf)
    first_loads = [nw_load]
    for h in range(heads):
        first_loads.append(load(q_hbm.at[:, pl.ds(h * FW, FW)], q_buf.at[h]))
    first_loads.append(load(att_hbm, att_buf))
    w_loads = {}
    for step in range(n):
        for way in range(2):
            dest = lax.rem(me + n - 1 - step, n) if way == 0 else lax.rem(me + 1 + step, n)
            start = pl.multiple_of(dest * (2 * HALF) + way * HALF, HALF)
            w_loads[step, way] = load(w_hbm.at[:, pl.ds(start, HALF)], w_buf.at[2 * step + way])

    barrier = pltpu.get_barrier_semaphore()
    for peer in targets:
        pl.semaphore_signal(barrier, inc=1, device_id={"head": peer}, device_id_type=MESH)
    pl.semaphore_wait(barrier, 2)

    def hop(step, sub, way):
        index = (step * SUBS + sub) * 2 + way
        return pltpu.make_async_remote_copy(
            src_ref=out_buf.at[step, sub, way], dst_ref=in_buf.at[step, sub, way],
            send_sem=send_sem.at[index], recv_sem=recv_sem.at[index],
            device_id={"head": targets[way]}, device_id_type=MESH,
        )

    for copy in first_loads:
        copy.wait()
    for way in range(2):
        w_loads[0, way].wait()

    def partial(step, sub, way):
        here = pl.ds(pl.multiple_of(sub * sub_rows, sub_rows), sub_rows)
        return dot(merged[here], w_buf[2 * step + way])

    def opening(sub, carry):
        here = pl.ds(pl.multiple_of(sub * sub_rows, sub_rows), sub_rows)
        for h in range(heads):
            q_rows = q_buf[h, here]
            gate_in = dot(q_rows, nw_buf[h, 0])
            up_in = dot(q_rows, nw_buf[h, 1])
            gated = (gate_in * sigmoid(gate_in) * up_in).astype(BF16)
            value = dot(gated, nw_buf[h, 2])
            norm = lax.rsqrt(jnp.mean(value * value, axis=1, keepdims=True) + 1e-06)
            merged[here, h * FW : (h + 1) * FW] = (
                att_buf[h, here].astype(F32) + value * norm
            ).astype(BF16)
        for way in range(2):
            out_buf[0, sub, way] = partial(0, sub, way).astype(BF16)
            hop(0, sub, way).start()
        return carry

    lax.fori_loop(0, SUBS, opening, 0)

    for step in range(1, n):
        for way in range(2):
            w_loads[step, way].wait()

        def middle(sub, carry, step=step):
            for way in range(2):
                mine = partial(step, sub, way)
                hop(step - 1, sub, way).wait_recv()
                value = (mine + in_buf[step - 1, sub, way].astype(F32)).astype(BF16)
                if step < n - 1:
                    out_buf[step, sub, way] = value
                    hop(step, sub, way).start()
                else:
                    here = pl.ds(pl.multiple_of(sub * sub_rows, sub_rows), sub_rows)
                    out_ref[here, way * HALF : (way + 1) * HALF] = value
            return carry

        lax.fori_loop(0, SUBS, middle, 0)

    for step in range(n - 1):

        def drain(sub, carry, step=step):
            for way in range(2):
                hop(step, sub, way).wait_send()
            return carry

        lax.fori_loop(0, SUBS, drain, 0)


def project(query, attended, new_weights, out_weight, n):
    rows, width = query.shape
    heads = width // FW
    sub_rows = rows // SUBS
    hbm = pl.BlockSpec(memory_space=pl.ANY)
    return pl.pallas_call(
        project_kernel,
        out_shape=jax.ShapeDtypeStruct((rows, 2 * HALF), BF16),
        in_specs=[hbm] * 4,
        out_specs=pl.BlockSpec(memory_space=pltpu.VMEM),
        scratch_shapes=[
            pltpu.VMEM((heads, rows, FW), BF16),
            pltpu.VMEM((heads, rows, FW), BF16),
            pltpu.VMEM((heads, 3, FW, FW), BF16),
            pltpu.VMEM((2 * n, width, HALF), BF16),
            pltpu.VMEM((rows, width), BF16),
            pltpu.VMEM((n - 1, SUBS, 2, sub_rows, HALF), BF16),
            pltpu.VMEM((n - 1, SUBS, 2, sub_rows, HALF), BF16),
            pltpu.SemaphoreType.DMA((2 * n + heads + 2,)),
            pltpu.SemaphoreType.DMA(((n - 1) * SUBS * 2,)),
            pltpu.SemaphoreType.DMA(((n - 1) * SUBS * 2,)),
        ],
        compiler_params=pltpu.CompilerParams(
            collective_id=1, has_side_effects=True, vmem_limit_bytes=56 * MIB
        ),
        name="project",
    )(query, attended, new_weights, out_weight)


def shards(query, keys, values, lr_code, fast_weights, out_weight):
    heads = fast_weights.shape[0]
    tokens_all = query.shape[0] * lax.axis_size("ctx")
    attended, pull, rate_sum = update(query, keys, values, lr_code.T, fast_weights)
    new_weights = renorm(
        rate_sum, pull.reshape(heads * 3, FW, FW), fast_weights.reshape(heads * 3, FW, FW), tokens_all
    ).reshape(heads, 3, FW, FW)
    layer_out = project(query, attended, new_weights, out_weight, lax.axis_size("head"))
    return (layer_out, new_weights)


def solution(mesh):
    placed = (
        P("ctx", "head"),
        P("ctx", "head"),
        P("ctx", "head"),
        P("ctx", "head"),
        P("head", None, None, None),
        P("head", None),
    )
    return jax.shard_map(
        shards,
        mesh=mesh,
        in_specs=placed,
        out_specs=(P("ctx", "head"), P("head", None, None, None)),
        check_vma=False,
    )
```

time: 347 us -> 146 us (0.42); the launches traced: 341 us -> 145 us
  Pallas kernels: 0 us -> 142 us
  local copies, waits for them, and re-layouts: 112 us -> 3.08 us
  waiting for transfers between devices: 80.2 us -> 0 us
  matrix products: 69.5 us -> 0 us
  other arithmetic: 48.9 us -> 0 us
  starting transfers between devices: 14.6 us -> 0 us
  between operations: 14.3 us -> 0.65 us
    pallas_call x0 -> x3, Pallas kernels: none -> 142 us  [the longest x1 79.3 us: project(): pl.pallas_call(project_kernel, out_shape=jax.ShapeDtypeStruct((rows, 2 *...]
    reduce_scatter x1 -> x0, waiting for transfers between devices: 80.2 us -> none  [shards(): lax.psum_scatter(partial_out.astype(jnp.bfloat16), 'head', scatter_dimens...]
    dynamic_update_slice x4 -> x0, local copies, waits for them, and re-layouts: 80 us -> none  [attention(): lax.map(one_block, jnp.arange(tok_rows // block_rows, dtype=jnp.int32))]
    dot_general x21 -> x0, matrix products: 69.5 us -> none  [the longest x2 16.3 us: one_block(): jnp.einsum('qhd,khd->hqk', q_block, k_block, preferred_element_type=jnp.f...]
    sub x2 -> x0, other arithmetic: 32.6 us -> none  [one_block(): exps = jnp.exp(scores - top_score)]
    unnamed x33 -> x1, local copies, waits for them, and re-layouts: 22.1 us -> 3.08 us
    all_to_all x1 -> x0, starting transfers between devices: 7.41 us -> none  [sent_to_all(): return lax.all_to_all(copies, axis, split_axis=0, concat_axis=0, tiled=True)]
    ppermute x2 -> x0, starting transfers between devices: 6.88 us -> none  [from_behind(): return lax.ppermute(block, axis, route)]
  transfers between devices with their start and end apart: 5 -> 0, of which waited for: 1 -> 0; matrix products, arithmetic and copies ran while one was open for 55% -> 0% of each run, Pallas kernels for 0% -> 0%
where the time goes in v1:
time: 146 us; the launch traced here: 145 us
  Pallas kernels  142 us (97%)
  local copies, waits for them, and re-layouts  3.08 us (2%)
    pallas_call x1, Pallas kernels, project(): pl.pallas_call(project_kernel, out_shape=jax.ShapeDtypeStruct((rows, 2 *...  79.3 us
    pallas_call x1, Pallas kernels, update(): pl.pallas_call(update_kernel, out_shape=(jax.ShapeDtypeStruct((heads, row...  55.5 us
    pallas_call x1, Pallas kernels, renorm(): pl.pallas_call(kernel, grid=(count,), out_shape=jax.ShapeDtypeStruct((cou...  6.82 us
    unnamed x1, local copies, waits for them, and re-layouts  3.08 us

profile of v1, /device:TPU:1, one launch (start us, length us, event | category | flops | bytes accessed | tf_op | source)
XLA Modules:
  0.0 145.3 jit_solution(14923148361839805878)
XLA Ops:
  0.6 55.5 %update.1 = (bf16[2,1024,512]{2,1,0:T(8,128)(2,1)}, bf16[2,1536,512]{2,1,0:T(8,128)(2,1)}, f32[2,128]{1,0:T(2,128)}) custom-call(bf16[1024,1024]{1,0:T(8,128)(2,1)} %q_hbm.3, bf16[1024,1024]{1,0:T(8,128)(2,1)} %k_hbm.1, bf16[1024,1024]{1,0:T(8,128)(2,1)} %v_hbm.1, s32[2,1024]{1,0:T(2,128)} %bitcast.8, bf16[2,3,512,512]{3,2,1,0:T(8,128)(2,1)} %fw_hbm.1), custom_call_target="tpu_custom_call" | custom-call | tf_op jit(solution)/shard_map/update/pallas_call | solution.py:289
  56.1 6.8 %renorm.1 = bf16[6,512,512]{2,1,0:T(8,128)(2,1)} custom-call(f32[2,128]{1,0:T(2,128)} %get-tuple-element.6.refs_0_, bf16[6,512,512]{2,1,0:T(8,128)(2,1)} %bitcast.7, bf16[6,512,512]{2,1,0:T(8,128)(2,1)} %bitcast.4), custom_call_target="tpu_custom_call" | custom-call | tf_op jit(solution)/shard_map/renorm/pallas_call | solution.py:348
  62.9 79.3 %project.1 = bf16[1024,1024]{1,0:T(8,128)(2,1)} custom-call(bf16[1024,1024]{1,0:T(8,128)(2,1)} %q_hbm.3, bf16[2,1024,512]{2,1,0:T(8,128)(2,1)} %get-tuple-element.5.att_hbm, bf16[2,3,512,512]{3,2,1,0:T(8,128)(2,1)} %bitcast.5, bf16[1024,4096]{1,0:T(8,128)(2,1)} %w_hbm.1), custom_call_target="tpu_custom_call" | custom-call | tf_op jit(solution)/shard_map/project/pallas_call | solution.py:470
  142.2 3.1 %copy.9 = bf16[1024,1024]{1,0:T(8,128)(2,1)} copy(bf16[1024,1024]{1,0:T(8,128)(2,1)} %project.1) | data formatting | bytes 4194304

commit v2 on v1

v2 whole, which is shorter than its diff:
```python
import math

import jax
import jax.numpy as jnp
from jax import lax
from jax.experimental import pallas as pl
from jax.experimental.pallas import tpu as pltpu
from jax.sharding import PartitionSpec as P

FW = 512
HEAD_DIM = 128
WINDOW = 256
BASE_RATE = 0.05
BLOCK = 256
F32 = jnp.float32
BF16 = jnp.bfloat16
MESH = pl.DeviceIdType.MESH
MIB = 1024 * 1024


def dot(left, right, left_dim=1, right_dim=0):
    return lax.dot_general(
        left, right, (((left_dim,), (right_dim,)), ((), ())), preferred_element_type=F32
    )


def sigmoid(x):
    return 0.5 * jnp.tanh(0.5 * x) + 0.5


RIM_K, RIM_V, CORE_G, CORE_R = 0, 1, 2, 3
X_A, X_B, X_R = 3, 6, 9
Y_A, Y_B, Y_R = 12, 15, 18
GY_A, GY_B, GX_A, GX_B = 21, 24, 27, 30
CORE_P = 34
COPIES = 35
RING = 4
SUBS = 4
HALF = 512


def layer_kernel(
    q_hbm, k_hbm, v_hbm, code_ref, fw_hbm, w_hbm,
    out_hbm, new_hbm,
    q_buf, k_buf, v_buf, fw_buf, base_buf, d_buf, gated_buf, pushed_buf,
    grad_out, grad_in, grad_sum, in_xa, in_xb, sum_a, sum_b, in_ya, in_yb,
    new_buf, rate_out, rate_in, att_buf, w_buf, merged, ring_out, ring_in, out_buf,
    load_sem, w_sem, store_sem, send_sem, recv_sem, ring_send, ring_recv,
):
    ctx = lax.axis_index("ctx")
    me = lax.axis_index("head")
    core = lax.rem(ctx, 2)
    chip = lax.div(ctx, 2)
    y = lax.rem(chip, RING)
    x = lax.div(chip, RING)
    contexts = lax.axis_size("ctx")
    groups = lax.axis_size("head")
    rows = k_hbm.shape[0]
    tokens_all = rows * contexts
    blocks = rows // BLOCK
    part = in_xa.shape[1]
    piece = in_ya.shape[1]
    half = grad_sum.shape[0] // 2
    heads = fw_buf.shape[0]

    def at(xx, yy, cc):
        return (xx * RING + yy) * 2 + cc

    partner = at(x, y, 1 - core)
    follower = lax.rem(ctx + 1, contexts)
    leader = lax.rem(ctx + contexts - 1, contexts)
    x_peer = [None] + [at(lax.rem(x + d, RING), y, core) for d in range(1, RING)]
    y_peer = [None] + [at(x, lax.rem(y + d, RING), core) for d in range(1, RING)]
    ring_peer = (lax.rem(me + 1, groups), lax.rem(me + groups - 1, groups))

    def load(src, dst, index):
        return pltpu.make_async_copy(src, dst, load_sem.at[index])

    first, second = 1 - core, core

    def lanes(head):
        return pl.ds(pl.multiple_of(head * FW, FW), FW)

    loads = {}
    for order, head in enumerate((first, second)):
        loads["w", order] = load(fw_hbm.at[head], fw_buf.at[head], 4 * order)
        loads["k", order] = load(
            k_hbm.at[:, lanes(head)], k_buf.at[head, pl.ds(WINDOW, rows)], 4 * order + 1
        )
        loads["v", order] = load(
            v_hbm.at[:, lanes(head)], v_buf.at[head, pl.ds(WINDOW, rows)], 4 * order + 2
        )
        loads["q", order] = load(q_hbm.at[:, lanes(head)], q_buf.at[head], 4 * order + 3)
    w_loads = {}
    for step in range(RING):
        for way in range(2):
            dest = lax.rem(me + groups - 1 - step, groups) if way == 0 else lax.rem(me + 1 + step, groups)
            start = pl.multiple_of(dest * (2 * HALF) + way * HALF, HALF)
            index = 2 * step + way
            w_loads[step, way] = pltpu.make_async_copy(
                w_hbm.at[:, pl.ds(start, HALF)], w_buf.at[index], w_sem.at[index]
            )
    for order in range(2):
        for name in ("w", "k", "v"):
            loads[name, order].start()

    barrier = pltpu.get_barrier_semaphore()
    ctx_peers = [follower, leader] + x_peer[1:] + y_peer[1:]
    for peer in ctx_peers:
        pl.semaphore_signal(barrier, inc=1, device_id={"ctx": peer}, device_id_type=MESH)
    for peer in ring_peer:
        pl.semaphore_signal(barrier, inc=1, device_id={"head": peer}, device_id_type=MESH)

    def remote(src, dst, index, peer):
        return pltpu.make_async_remote_copy(
            src_ref=src, dst_ref=dst, send_sem=send_sem.at[index], recv_sem=recv_sem.at[index],
            device_id={"ctx": peer}, device_id_type=MESH,
        )

    sent = []

    def send(copy):
        copy.start()
        sent.append(copy)
        return copy

    def train(head):
        def tokens(t, carry):
            start = pl.multiple_of(t * BLOCK, BLOCK)
            k_rows = k_buf[head, pl.ds(start + WINDOW, BLOCK)]
            v_rows = v_buf[head, pl.ds(start + WINDOW, BLOCK)].astype(F32)
            code_row = code_ref[pl.ds(head, 1), pl.ds(start, BLOCK)].astype(F32) * 2.0 ** (-14)
            column = jnp.transpose(jnp.broadcast_to(code_row, (8, BLOCK)))[:, 0:1]
            pushed = (column * v_rows).astype(BF16)
            gate_in = dot(k_rows, fw_buf[head, 0])
            up_in = dot(k_rows, fw_buf[head, 1])
            back = dot(pushed, fw_buf[head, 2], 1, 1)
            s = sigmoid(gate_in)
            gs = gate_in * s
            here = pl.ds(start, BLOCK)
            pushed_buf[here] = pushed
            gated_buf[here] = (gs * up_in).astype(BF16)
            d_buf[here, 0:FW] = (back * up_in * (s * (1.0 + gate_in * (1.0 - s)))).astype(BF16)
            d_buf[here, FW : 2 * FW] = (back * gs).astype(BF16)
            return carry

        lax.fori_loop(0, blocks, tokens, 0)

    def pulls(head, put):
        k_own = k_buf.at[head, pl.ds(WINDOW, rows)]
        for i in range(2 * FW // BLOCK):
            cols = pl.ds(i * BLOCK, BLOCK)
            put(cols, dot(d_buf[:, cols], k_own[...], 0, 0))
        for i in range(FW // BLOCK):
            cols = pl.ds(i * BLOCK, BLOCK)
            put(pl.ds(2 * FW + i * BLOCK, BLOCK), dot(pushed_buf[:, cols], gated_buf[...], 0, 0))

    def put_out(where, value):
        grad_out[where] = value.astype(BF16)

    def put_sum(where, value):
        grad_sum[where] = (value + grad_in[where].astype(F32)).astype(BF16)

    for name in ("w", "k", "v"):
        loads[name, 0].wait()
    train(first)
    for name in ("w", "k", "v"):
        loads[name, 1].wait()
    for order in range(2):
        loads["q", order].start()
    for copy in w_loads.values():
        copy.start()
    pl.semaphore_wait(barrier, len(ctx_peers) + len(ring_peer))
    rim = [
        send(remote(k_buf.at[:, pl.ds(rows, WINDOW)], k_buf.at[:, pl.ds(0, WINDOW)], RIM_K, follower)),
        send(remote(v_buf.at[:, pl.ds(rows, WINDOW)], v_buf.at[:, pl.ds(0, WINDOW)], RIM_V, follower)),
    ]
    pulls(first, put_out)
    core_grad = send(remote(grad_out, grad_in, CORE_G, partner))
    rate = code_ref[...].astype(F32) * 2.0 ** (-14)
    rate_out[0] = jnp.broadcast_to(jnp.sum(rate, axis=1, keepdims=True), rate_out.shape[1:])
    core_rate = send(remote(rate_out.at[0], rate_in.at[0], CORE_R, partner))
    train(second)
    core_rate.wait_recv()
    rate_out[1] = rate_out[0] + rate_in[0]
    core_grad.wait_recv()
    pulls(second, put_sum)

    def aligned(start, size):
        return pl.ds(pl.multiple_of(start, 16), size)

    def ring_to(index):
        return lax.rem(index, RING)

    out_x = []
    for d in range(1, RING):
        out_x.append(send(remote(
            grad_sum.at[aligned(ring_to(x + d) * part, part)], in_xa.at[d - 1], X_A + d, x_peer[d])))
        out_x.append(send(remote(
            grad_sum.at[aligned(half + ring_to(y + d) * part, part)], in_xb.at[d - 1], X_B + d, y_peer[d])))
        out_x.append(send(remote(rate_out.at[1], rate_in.at[d], X_R + d, x_peer[d])))

    for m in range(3):
        base_buf[m * FW : (m + 1) * FW] = jnp.transpose(fw_buf[core, m])
    for copy in rim:
        copy.wait_recv()
    for order in range(2):
        loads["q", order].wait()

    row_id = lax.broadcasted_iota(jnp.int32, (BLOCK, BLOCK), 0)
    col_id = lax.broadcasted_iota(jnp.int32, (BLOCK, BLOCK), 1)
    scale = math.log2(math.e) / math.sqrt(HEAD_DIM)

    def attend(unit, carry):
        head = lax.div(unit, blocks)
        block = lax.rem(unit, blocks)
        start = pl.multiple_of(block * BLOCK, BLOCK)
        unseen = jnp.where((ctx == 0) & (block == 0), -1e30, 0.0).astype(F32)
        causal = col_id <= row_id
        for j in range(FW // HEAD_DIM):
            cols = pl.ds(j * HEAD_DIM, HEAD_DIM)
            q_rows = q_buf[head, pl.ds(start, BLOCK), cols]
            scores = dot(q_rows, k_buf[head, pl.ds(start, 2 * BLOCK), cols], 1, 1)
            live = jnp.where(causal, scores[:, BLOCK:], scores[:, :BLOCK] + unseen)
            top = jnp.max(live, axis=1, keepdims=True)
            exps = jnp.exp2((live - top) * scale)
            old = jnp.where(causal, 0.0, exps).astype(BF16)
            new = jnp.where(causal, exps, 0.0).astype(BF16)
            ones = jnp.ones((BLOCK, HEAD_DIM), BF16)
            v_old = jnp.concatenate([v_buf[head, pl.ds(start, BLOCK), cols], ones], 1)
            v_new = jnp.concatenate([v_buf[head, pl.ds(start + BLOCK, BLOCK), cols], ones], 1)
            both = dot(old, v_old) + dot(new, v_new)
            att_buf[head, pl.ds(start, BLOCK), cols] = (
                both[:, :HEAD_DIM] / both[:, HEAD_DIM:]
            ).astype(BF16)
        return carry

    units = 2 * blocks
    lax.fori_loop(0, units // 2, attend, 0)

    for copy in out_x:
        copy.wait_recv()

    def total(own, others):
        value = own.astype(F32)
        for i in range(RING - 1):
            value = value + others[i].astype(F32)
        return value

    sum_a[...] = total(grad_sum[aligned(x * part, part)], in_xa).astype(BF16)
    sum_b[...] = total(grad_sum[aligned(half + y * part, part)], in_xb).astype(BF16)
    rate_out[2] = rate_out[1] + rate_in[1] + rate_in[2] + rate_in[3]

    out_y = []
    for d in range(1, RING):
        out_y.append(send(remote(
            sum_a.at[aligned(ring_to(y + d) * piece, piece)], in_ya.at[d - 1], Y_A + d, y_peer[d])))
        out_y.append(send(remote(
            sum_b.at[aligned(ring_to(x + d) * piece, piece)], in_yb.at[d - 1], Y_B + d, x_peer[d])))
        out_y.append(send(remote(rate_out.at[2], rate_in.at[RING - 1 + d], Y_R + d, y_peer[d])))
    lax.fori_loop(units // 2, units // 2 + 1, attend, 0)
    for copy in out_y:
        copy.wait_recv()
    rate_out[3] = rate_out[2] + rate_in[4] + rate_in[5] + rate_in[6]
    step_size = BASE_RATE / (math.sqrt(tokens_all) * (rate_out[3, pl.ds(core, 1), 0:1] / tokens_all))

    def renorm(where, pull):
        base = base_buf[where].astype(F32)
        updated = base + step_size * pull
        old_norm = jnp.sqrt(jnp.sum(base * base, axis=1, keepdims=True) + 1e-06)
        new_norm = jnp.sqrt(jnp.sum(updated * updated, axis=1, keepdims=True) + 1e-06)
        new_buf[core, where] = (updated * (old_norm / new_norm)).astype(BF16)

    own_a = aligned(x * part + y * piece, piece)
    own_b = aligned(half + y * part + x * piece, piece)
    renorm(own_a, total(sum_a[aligned(y * piece, piece)], in_ya))
    renorm(own_b, total(sum_b[aligned(x * piece, piece)], in_yb))

    back_y = []
    for d in range(1, RING):
        mine_a, mine_b = new_buf.at[core, own_a], new_buf.at[core, own_b]
        back_y.append(send(remote(mine_a, mine_a, GY_A + d, y_peer[d])))
        back_y.append(send(remote(mine_b, mine_b, GY_B + d, x_peer[d])))
    lax.fori_loop(units // 2 + 1, units // 2 + 2, attend, 0)
    for copy in back_y:
        copy.wait_recv()

    back_x = []
    for d in range(1, RING):
        mine_a = new_buf.at[core, aligned(x * part, part)]
        mine_b = new_buf.at[core, aligned(half + y * part, part)]
        back_x.append(send(remote(mine_a, mine_a, GX_A + d, x_peer[d])))
        back_x.append(send(remote(mine_b, mine_b, GX_B + d, y_peer[d])))
    lax.fori_loop(units // 2 + 2, units, attend, 0)
    for copy in w_loads.values():
        copy.wait()
    for copy in back_x:
        copy.wait_recv()
    across = send(remote(new_buf.at[core], new_buf.at[core], CORE_P, partner))
    across.wait_recv()
    store_new = pltpu.make_async_copy(new_buf, new_hbm, store_sem.at[SUBS])
    store_new.start()

    sub_rows = rows // SUBS

    def hop(step, sub, way):
        index = (step * SUBS + sub) * 2 + way
        return pltpu.make_async_remote_copy(
            src_ref=ring_out.at[step, sub, way], dst_ref=ring_in.at[step, sub, way],
            send_sem=ring_send.at[index], recv_sem=ring_recv.at[index],
            device_id={"head": ring_peer[way]}, device_id_type=MESH,
        )

    def chunk(sub):
        return pl.ds(pl.multiple_of(sub * sub_rows, sub_rows), sub_rows)

    def partial(step, sub, way):
        return dot(merged[chunk(sub)], w_buf[2 * step + way])

    def opening(sub, carry):
        here = chunk(sub)
        for h in range(heads):
            q_rows = q_buf[h, here]
            gate_in = dot(q_rows, new_buf[h, 0:FW], 1, 1)
            up_in = dot(q_rows, new_buf[h, FW : 2 * FW], 1, 1)
            gated = (gate_in * sigmoid(gate_in) * up_in).astype(BF16)
            value = dot(gated, new_buf[h, 2 * FW : 3 * FW], 1, 1)
            norm = lax.rsqrt(jnp.mean(value * value, axis=1, keepdims=True) + 1e-06)
            merged[here, h * FW : (h + 1) * FW] = (
                att_buf[h, here].astype(F32) + value * norm
            ).astype(BF16)
        for way in range(2):
            ring_out[0, sub, way] = partial(0, sub, way).astype(BF16)
            hop(0, sub, way).start()
        return carry

    lax.fori_loop(0, SUBS, opening, 0)

    def store_out(sub):
        return pltpu.make_async_copy(out_buf.at[chunk(sub)], out_hbm.at[chunk(sub)], store_sem.at[sub])

    for step in range(1, RING):

        def middle(sub, carry, step=step):
            for way in range(2):
                mine = partial(step, sub, way)
                hop(step - 1, sub, way).wait_recv()
                value = (mine + ring_in[step - 1, sub, way].astype(F32)).astype(BF16)
                if step < RING - 1:
                    ring_out[step, sub, way] = value
                    hop(step, sub, way).start()
                else:
                    out_buf[chunk(sub), way * HALF : (way + 1) * HALF] = value
            if step == RING - 1:
                store_out(sub).start()
            return carry

        lax.fori_loop(0, SUBS, middle, 0)

    for copy in sent:
        copy.wait_send()
    for step in range(RING - 1):

        def drain(sub, carry, step=step):
            for way in range(2):
                hop(step, sub, way).wait_send()
            return carry

        lax.fori_loop(0, SUBS, drain, 0)
    for sub in range(SUBS):
        store_out(sub).wait()
    store_new.wait()


def layer(query, keys, values, code_t, fast_weights, out_weight):
    rows, width = query.shape
    heads = width // FW
    pulled = 3 * FW
    part = pulled // 2 // RING
    piece = part // RING
    sub_rows = rows // SUBS
    hops = (RING - 1) * SUBS * 2
    hbm = pl.BlockSpec(memory_space=pl.ANY)
    vmem = pl.BlockSpec(memory_space=pltpu.VMEM)
    return pl.pallas_call(
        layer_kernel,
        out_shape=(
            jax.ShapeDtypeStruct((rows, 2 * HALF), BF16),
            jax.ShapeDtypeStruct((heads, pulled, FW), BF16),
        ),
        in_specs=[hbm, hbm, hbm, vmem, hbm, hbm],
        out_specs=(hbm, hbm),
        scratch_shapes=[
            pltpu.VMEM((heads, rows, FW), BF16),
            pltpu.VMEM((heads, rows + WINDOW, FW), BF16),
            pltpu.VMEM((heads, rows + WINDOW, FW), BF16),
            pltpu.VMEM((heads, 3, FW, FW), BF16),
            pltpu.VMEM((pulled, FW), BF16),
            pltpu.VMEM((rows, 2 * FW), BF16),
            pltpu.VMEM((rows, FW), BF16),
            pltpu.VMEM((rows, FW), BF16),
            pltpu.VMEM((pulled, FW), BF16),
            pltpu.VMEM((pulled, FW), BF16),
            pltpu.VMEM((pulled, FW), BF16),
            pltpu.VMEM((RING - 1, part, FW), BF16),
            pltpu.VMEM((RING - 1, part, FW), BF16),
            pltpu.VMEM((part, FW), BF16),
            pltpu.VMEM((part, FW), BF16),
            pltpu.VMEM((RING - 1, piece, FW), BF16),
            pltpu.VMEM((RING - 1, piece, FW), BF16),
            pltpu.VMEM((heads, pulled, FW), BF16),
            pltpu.VMEM((4, heads, 128), F32),
            pltpu.VMEM((7, heads, 128), F32),
            pltpu.VMEM((heads, rows, FW), BF16),
            pltpu.VMEM((2 * RING, width, HALF), BF16),
            pltpu.VMEM((rows, width), BF16),
            pltpu.VMEM((RING - 1, SUBS, 2, sub_rows, HALF), BF16),
            pltpu.VMEM((RING - 1, SUBS, 2, sub_rows, HALF), BF16),
            pltpu.VMEM((rows, 2 * HALF), BF16),
            pltpu.SemaphoreType.DMA((8,)),
            pltpu.SemaphoreType.DMA((2 * RING,)),
            pltpu.SemaphoreType.DMA((SUBS + 1,)),
            pltpu.SemaphoreType.DMA((COPIES,)),
            pltpu.SemaphoreType.DMA((COPIES,)),
            pltpu.SemaphoreType.DMA((hops,)),
            pltpu.SemaphoreType.DMA((hops,)),
        ],
        compiler_params=pltpu.CompilerParams(
            collective_id=0, has_side_effects=True, vmem_limit_bytes=60 * MIB
        ),
        name="layer",
    )(query, keys, values, code_t, fast_weights, out_weight)


def finish_kernel(out_ref, turned_ref, final_ref, new_ref):
    final_ref[...] = out_ref[...]
    for h in range(new_ref.shape[0]):
        for m in range(3):
            new_ref[h, m] = jnp.transpose(turned_ref[h, m * FW : (m + 1) * FW])


def finish(out, turned):
    rows, width = out.shape
    heads, pulled, inner = turned.shape
    steps = 4
    out_spec = pl.BlockSpec((rows // steps, width), lambda i: (i, 0))
    return pl.pallas_call(
        finish_kernel,
        grid=(steps,),
        out_shape=(
            jax.ShapeDtypeStruct(out.shape, BF16),
            jax.ShapeDtypeStruct((heads, 3, inner, FW), BF16),
        ),
        in_specs=[out_spec, pl.BlockSpec((heads, pulled, inner // steps), lambda i: (0, 0, i))],
        out_specs=(out_spec, pl.BlockSpec((heads, 3, inner // steps, FW), lambda i: (0, 0, i, 0))),
        name="finish",
    )(out, turned)


def shards(query, keys, values, lr_code, fast_weights, out_weight):
    out, turned = layer(query, keys, values, lr_code.T, fast_weights, out_weight)
    return finish(out, turned)


def solution(mesh):
    placed = (
        P("ctx", "head"),
        P("ctx", "head"),
        P("ctx", "head"),
        P("ctx", "head"),
        P("head", None, None, None),
        P("head", None),
    )
    return jax.shard_map(
        shards,
        mesh=mesh,
        in_specs=placed,
        out_specs=(P("ctx", "head"), P("head", None, None, None)),
        check_vma=False,
    )
```

time: 146 us -> 137 us (0.938)
  Pallas kernels: 142 us -> 136 us
  local copies, waits for them, and re-layouts: 3.08 us -> 0 us
    pallas_call x3 -> x2, Pallas kernels: 142 us -> 136 us  [the longest x1 131 us: layer(): pl.pallas_call(layer_kernel, out_shape=(jax.ShapeDtypeStruct((rows, 2 * H...]
    unnamed x1 -> x0, local copies, waits for them, and re-layouts: 3.08 us -> none
where the time goes in v2:
time: 137 us
  Pallas kernels  136 us (99%)
    pallas_call x1, Pallas kernels, layer(): pl.pallas_call(layer_kernel, out_shape=(jax.ShapeDtypeStruct((rows, 2 * H...  131 us
    pallas_call x1, Pallas kernels, finish(): pl.pallas_call(finish_kernel, grid=(steps,), out_shape=(jax.ShapeDtypeStr...  5.51 us

profile of v2, /device:TPU:1, one launch (start us, length us, event | category | flops | bytes accessed | tf_op | source)
XLA Modules:
  0.0 137.1 jit_solution(15414646366094462231)
XLA Ops:
  0.6 130.9 %layer.1 = (bf16[1024,1024]{1,0:T(8,128)(2,1)}, bf16[2,1536,512]{2,1,0:T(8,128)(2,1)}) custom-call(bf16[1024,1024]{1,0:T(8,128)(2,1)} %q_hbm.1, bf16[1024,1024]{1,0:T(8,128)(2,1)} %k_hbm.1, bf16[1024,1024]{1,0:T(8,128)(2,1)} %v_hbm.1, s32[2,1024]{1,0:T(2,128)} %bitcast.1, bf16[2,3,512,512]{3,2,1,0:T(8,128)(2,1)} %fw_hbm.1, bf16[1024,4096]{1,0:T(8,128)(2,1)} %w_hbm.1), custom_call_target="tpu_custom_call" | custom-call | tf_op jit(solution)/shard_map/layer/pallas_call | solution.py:385
  131.5 5.5 %finish.1 = (bf16[1024,1024]{1,0:T(8,128)(2,1)}, bf16[2,3,512,512]{3,2,1,0:T(8,128)(2,1)}) custom-call(bf16[1024,1024]{1,0:T(8,128)(2,1)} %get-tuple-element.4.out_ref, bf16[2,1536,512]{2,1,0:T(8,128)(2,1)} %get-tuple-element.5.turned_ref), custom_call_target="tpu_custom_call" | custom-call | tf_op jit(solution)/shard_map/finish/pallas_call | solution.py:447

commit v3 on v2

--- a/solution.py
+++ b/solution.py
@@ -33,9 +33,13 @@
 Y_A, Y_B, Y_R = 12, 15, 18
 GY_A, GY_B, GX_A, GX_B = 21, 24, 27, 30
 CORE_P = 34
-COPIES = 35
+PAIR_Q, PAIR_ATT, WZ_A, WZ_B = 35, 36, 37, 38
+W1_A, W1_B, W2_A, W2_B, W_CORE = 38, 41, 44, 47, 51
+NZ_A, NZ_B = 52, 53
+HY_A, HY_B, HX_A, HX_B, H_CORE = 53, 56, 59, 62, 66
+COPIES = 67
 RING = 4
-SUBS = 4
+SUBS = 2
 HALF = 512
 
 
@@ -45,7 +49,8 @@
     q_buf, k_buf, v_buf, fw_buf, base_buf, d_buf, gated_buf, pushed_buf,
     grad_out, grad_in, grad_sum, in_xa, in_xb, sum_a, sum_b, in_ya, in_yb,
     new_buf, rate_out, rate_in, att_buf, w_buf, merged, ring_out, ring_in, out_buf,
-    load_sem, w_sem, store_sem, send_sem, recv_sem, ring_send, ring_recv,
+    q_pair, att_pair, w_pair, new_pair, pair_out, pair_in,
+    load_sem, w_sem, store_sem, send_sem, recv_sem, ring_send, ring_recv, pair_send, pair_recv,
 ):
     ctx = lax.axis_index("ctx")
     me = lax.axis_index("head")
@@ -71,6 +76,7 @@
     leader = lax.rem(ctx + contexts - 1, contexts)
     x_peer = [None] + [at(lax.rem(x + d, RING), y, core) for d in range(1, RING)]
     y_peer = [None] + [at(x, lax.rem(y + d, RING), core) for d in range(1, RING)]
+    opposite = lax.rem(me + 2, groups)
     ring_peer = (lax.rem(me + 1, groups), lax.rem(me + groups - 1, groups))
 
     def load(src, dst, index):
@@ -103,18 +109,24 @@
     for order in range(2):
         for name in ("w", "k", "v"):
             loads[name, order].start()
+    for step in range(2):
+        for way in range(2):
+            w_loads[step, way].start()
+    for order in range(2):
+        loads["q", order].start()
 
     barrier = pltpu.get_barrier_semaphore()
     ctx_peers = [follower, leader] + x_peer[1:] + y_peer[1:]
     for peer in ctx_peers:
         pl.semaphore_signal(barrier, inc=1, device_id={"ctx": peer}, device_id_type=MESH)
-    for peer in ring_peer:
+    head_peers = ring_peer + (opposite,)
+    for peer in head_peers:
         pl.semaphore_signal(barrier, inc=1, device_id={"head": peer}, device_id_type=MESH)
 
-    def remote(src, dst, index, peer):
+    def remote(src, dst, index, peer, axis="ctx"):
         return pltpu.make_async_remote_copy(
             src_ref=src, dst_ref=dst, send_sem=send_sem.at[index], recv_sem=recv_sem.at[index],
-            device_id={"ctx": peer}, device_id_type=MESH,
+            device_id={axis: peer}, device_id_type=MESH,
         )
 
     sent = []
@@ -166,29 +178,50 @@
     train(first)
     for name in ("w", "k", "v"):
         loads[name, 1].wait()
-    for order in range(2):
-        loads["q", order].start()
-    for copy in w_loads.values():
-        copy.start()
-    pl.semaphore_wait(barrier, len(ctx_peers) + len(ring_peer))
+    for step in range(2, RING):
+        for way in range(2):
+            w_loads[step, way].start()
+    pl.semaphore_wait(barrier, len(ctx_peers) + len(head_peers))
     rim = [
         send(remote(k_buf.at[:, pl.ds(rows, WINDOW)], k_buf.at[:, pl.ds(0, WINDOW)], RIM_K, follower)),
         send(remote(v_buf.at[:, pl.ds(rows, WINDOW)], v_buf.at[:, pl.ds(0, WINDOW)], RIM_V, follower)),
     ]
+    shared = rows // 2
+    for step in range(2):
+        for way in range(2):
+            w_loads[step, way].wait()
+    slice_rows = w_buf.shape[1] // contexts
+
+    def aligned(start, size):
+        return pl.ds(pl.multiple_of(start, 16), size)
+
+    w_own_a = aligned(((core * RING + x) * RING + y) * slice_rows, slice_rows)
+    w_own_b = aligned(((core * RING + y) * RING + x) * slice_rows, slice_rows)
+    one, two = pl.ds(0, 2), pl.ds(2, 2)
+    w_z = [
+        send(remote(w_buf.at[one, w_own_a], w_pair.at[one, w_own_a], WZ_A, opposite, "head")),
+        send(remote(w_buf.at[two, w_own_b], w_pair.at[two, w_own_b], WZ_B, opposite, "head")),
+    ]
+    for order in range(2):
+        loads["q", order].wait()
+    pair_q = send(remote(q_buf.at[:, pl.ds(shared, shared)], q_pair, PAIR_Q, opposite, "head"))
     pulls(first, put_out)
     core_grad = send(remote(grad_out, grad_in, CORE_G, partner))
     rate = code_ref[...].astype(F32) * 2.0 ** (-14)
     rate_out[0] = jnp.broadcast_to(jnp.sum(rate, axis=1, keepdims=True), rate_out.shape[1:])
     core_rate = send(remote(rate_out.at[0], rate_in.at[0], CORE_R, partner))
+    for copy in w_z:
+        copy.wait_recv()
+    w_1 = []
+    for d in range(1, RING):
+        w_1.append(send(remote(w_pair.at[one, w_own_a], w_pair.at[one, w_own_a], W1_A + d, y_peer[d])))
+        w_1.append(send(remote(w_pair.at[two, w_own_b], w_pair.at[two, w_own_b], W1_B + d, x_peer[d])))
     train(second)
     core_rate.wait_recv()
     rate_out[1] = rate_out[0] + rate_in[0]
     core_grad.wait_recv()
     pulls(second, put_sum)
 
-    def aligned(start, size):
-        return pl.ds(pl.multiple_of(start, 16), size)
-
     def ring_to(index):
         return lax.rem(index, RING)
 
@@ -204,16 +237,14 @@
         base_buf[m * FW : (m + 1) * FW] = jnp.transpose(fw_buf[core, m])
     for copy in rim:
         copy.wait_recv()
-    for order in range(2):
-        loads["q", order].wait()
 
     row_id = lax.broadcasted_iota(jnp.int32, (BLOCK, BLOCK), 0)
     col_id = lax.broadcasted_iota(jnp.int32, (BLOCK, BLOCK), 1)
     scale = math.log2(math.e) / math.sqrt(HEAD_DIM)
 
     def attend(unit, carry):
-        head = lax.div(unit, blocks)
-        block = lax.rem(unit, blocks)
+        head = lax.div(lax.rem(unit, blocks), 2)
+        block = lax.rem(unit, 2) + 2 * (1 - lax.div(unit, blocks))
         start = pl.multiple_of(block * BLOCK, BLOCK)
         unseen = jnp.where((ctx == 0) & (block == 0), -1e30, 0.0).astype(F32)
         causal = col_id <= row_id
@@ -237,6 +268,7 @@
 
     units = 2 * blocks
     lax.fori_loop(0, units // 2, attend, 0)
+    pair_att = send(remote(att_buf.at[:, pl.ds(shared, shared)], att_pair, PAIR_ATT, opposite, "head"))
 
     for copy in out_x:
         copy.wait_recv()
@@ -281,6 +313,10 @@
         mine_a, mine_b = new_buf.at[core, own_a], new_buf.at[core, own_b]
         back_y.append(send(remote(mine_a, mine_a, GY_A + d, y_peer[d])))
         back_y.append(send(remote(mine_b, mine_b, GY_B + d, x_peer[d])))
+    new_z = [
+        send(remote(new_buf.at[core, own_a], new_pair.at[core, own_a], NZ_A, opposite, "head")),
+        send(remote(new_buf.at[core, own_b], new_pair.at[core, own_b], NZ_B, opposite, "head")),
+    ]
     lax.fori_loop(units // 2 + 1, units // 2 + 2, attend, 0)
     for copy in back_y:
         copy.wait_recv()
@@ -291,17 +327,27 @@
         mine_b = new_buf.at[core, aligned(half + y * part, part)]
         back_x.append(send(remote(mine_a, mine_a, GX_A + d, x_peer[d])))
         back_x.append(send(remote(mine_b, mine_b, GX_B + d, y_peer[d])))
+    for copy in w_1:
+        copy.wait_recv()
+    part_rows = slice_rows * RING
+    w_2 = []
+    for d in range(1, RING):
+        w_x = w_pair.at[one, aligned((core * RING + x) * part_rows, part_rows)]
+        w_y = w_pair.at[two, aligned((core * RING + y) * part_rows, part_rows)]
+        w_2.append(send(remote(w_x, w_x, W2_A + d, x_peer[d])))
+        w_2.append(send(remote(w_y, w_y, W2_B + d, y_peer[d])))
     lax.fori_loop(units // 2 + 2, units, attend, 0)
-    for copy in w_loads.values():
-        copy.wait()
+    for step in range(2, RING):
+        for way in range(2):
+            w_loads[step, way].wait()
     for copy in back_x:
         copy.wait_recv()
     across = send(remote(new_buf.at[core], new_buf.at[core], CORE_P, partner))
     across.wait_recv()
-    store_new = pltpu.make_async_copy(new_buf, new_hbm, store_sem.at[SUBS])
+    store_new = pltpu.make_async_copy(new_buf, new_hbm, store_sem.at[2 * SUBS])
     store_new.start()
 
-    sub_rows = rows // SUBS
+    sub_rows = shared // SUBS
 
     def hop(step, sub, way):
         index = (step * SUBS + sub) * 2 + way
@@ -311,37 +357,51 @@
             device_id={"head": ring_peer[way]}, device_id_type=MESH,
         )
 
+    def pair_hop(sub, way):
+        index = sub * 2 + way
+        return pltpu.make_async_remote_copy(
+            src_ref=pair_out.at[sub, way], dst_ref=pair_in.at[sub, way],
+            send_sem=pair_send.at[index], recv_sem=pair_recv.at[index],
+            device_id={"head": ring_peer[way]}, device_id_type=MESH,
+        )
+
     def chunk(sub):
         return pl.ds(pl.multiple_of(sub * sub_rows, sub_rows), sub_rows)
 
     def partial(step, sub, way):
         return dot(merged[chunk(sub)], w_buf[2 * step + way])
 
-    def opening(sub, carry):
+    merged_pair = d_buf
+
+    def partial_pair(step, sub, way, slot):
+        theirs = dot(merged_pair[chunk(sub), 0 : heads * FW], w_pair[slot])
+        return partial(step, SUBS + sub, way) + theirs
+
+    def apply(q_rows, weights, attended, h):
+        gate_in = dot(q_rows, weights[h, 0:FW], 1, 1)
+        up_in = dot(q_rows, weights[h, FW : 2 * FW], 1, 1)
+        gated = (gate_in * sigmoid(gate_in) * up_in).astype(BF16)
+        value = dot(gated, weights[h, 2 * FW : 3 * FW], 1, 1)
+        norm = lax.rsqrt(jnp.mean(value * value, axis=1, keepdims=True) + 1e-06)
+        return (attended.astype(F32) + value * norm).astype(BF16)
+
+    def apply_own(sub):
         here = chunk(sub)
         for h in range(heads):
-            q_rows = q_buf[h, here]
-            gate_in = dot(q_rows, new_buf[h, 0:FW], 1, 1)
-            up_in = dot(q_rows, new_buf[h, FW : 2 * FW], 1, 1)
-            gated = (gate_in * sigmoid(gate_in) * up_in).astype(BF16)
-            value = dot(gated, new_buf[h, 2 * FW : 3 * FW], 1, 1)
-            norm = lax.rsqrt(jnp.mean(value * value, axis=1, keepdims=True) + 1e-06)
-            merged[here, h * FW : (h + 1) * FW] = (
-                att_buf[h, here].astype(F32) + value * norm
-            ).astype(BF16)
+            merged[here, h * FW : (h + 1) * FW] = apply(q_buf[h, here], new_buf, att_buf[h, here], h)
+
+    def opening(sub, carry):
+        apply_own(sub)
         for way in range(2):
             ring_out[0, sub, way] = partial(0, sub, way).astype(BF16)
             hop(0, sub, way).start()
         return carry
 
-    lax.fori_loop(0, SUBS, opening, 0)
-
     def store_out(sub):
         return pltpu.make_async_copy(out_buf.at[chunk(sub)], out_hbm.at[chunk(sub)], store_sem.at[sub])
 
-    for step in range(1, RING):
-
-        def middle(sub, carry, step=step):
+    def round_ring(step):
+        def middle(sub, carry):
             for way in range(2):
                 mine = partial(step, sub, way)
                 hop(step - 1, sub, way).wait_recv()
@@ -357,17 +417,82 @@
 
         lax.fori_loop(0, SUBS, middle, 0)
 
+    lax.fori_loop(0, SUBS, opening, 0)
+
+    for copy in new_z:
+        copy.wait_recv()
+    pair_y = []
+    for d in range(1, RING):
+        mine_a, mine_b = new_pair.at[core, own_a], new_pair.at[core, own_b]
+        pair_y.append(send(remote(mine_a, mine_a, HY_A + d, y_peer[d])))
+        pair_y.append(send(remote(mine_b, mine_b, HY_B + d, x_peer[d])))
+
+    def apply_shared(sub, carry):
+        apply_own(SUBS + sub)
+        return carry
+
+    lax.fori_loop(0, SUBS, apply_shared, 0)
+    for copy in pair_y:
+        copy.wait_recv()
+    pair_x = []
+    for d in range(1, RING):
+        mine_a = new_pair.at[core, aligned(x * part, part)]
+        mine_b = new_pair.at[core, aligned(half + y * part, part)]
+        pair_x.append(send(remote(mine_a, mine_a, HX_A + d, x_peer[d])))
+        pair_x.append(send(remote(mine_b, mine_b, HX_B + d, y_peer[d])))
+
+    round_ring(1)
+    for copy in w_2:
+        copy.wait_recv()
+    w_half = w_pair.at[:, aligned(core * RING * part_rows, RING * part_rows)]
+    w_across = send(remote(w_half, w_half, W_CORE, partner))
+    round_ring(2)
+    for copy in pair_x:
+        copy.wait_recv()
+    pair_across = send(remote(new_pair.at[core], new_pair.at[core], H_CORE, partner))
+    pair_q.wait_recv()
+    pair_att.wait_recv()
+    w_across.wait_recv()
+    pair_across.wait_recv()
+
+    def opening_pair(sub, carry):
+        here = chunk(sub)
+        for h in range(heads):
+            merged_pair[here, h * FW : (h + 1) * FW] = apply(
+                q_pair[h, here], new_pair, att_pair[h, here], h
+            )
+        for way in range(2):
+            pair_out[sub, way] = partial_pair(2, sub, way, way).astype(BF16)
+            pair_hop(sub, way).start()
+        return carry
+
+    lax.fori_loop(0, SUBS, opening_pair, 0)
+    round_ring(3)
+
+    def closing_pair(sub, carry):
+        for way in range(2):
+            mine = partial_pair(3, sub, way, 2 + way)
+            pair_hop(sub, way).wait_recv()
+            out_buf[chunk(SUBS + sub), way * HALF : (way + 1) * HALF] = (
+                mine + pair_in[sub, way].astype(F32)
+            ).astype(BF16)
+        store_out(SUBS + sub).start()
+        return carry
+
+    lax.fori_loop(0, SUBS, closing_pair, 0)
+
     for copy in sent:
         copy.wait_send()
-    for step in range(RING - 1):
-
-        def drain(sub, carry, step=step):
-            for way in range(2):
+
+    def drain(sub, carry):
+        for way in range(2):
+            for step in range(RING - 1):
                 hop(step, sub, way).wait_send()
-            return carry
-
-        lax.fori_loop(0, SUBS, drain, 0)
-    for sub in range(SUBS):
+            pair_hop(sub, way).wait_send()
+        return carry
+
+    lax.fori_loop(0, SUBS, drain, 0)
+    for sub in range(2 * SUBS):
         store_out(sub).wait()
     store_new.wait()
 
@@ -378,7 +503,8 @@
     pulled = 3 * FW
     part = pulled // 2 // RING
     piece = part // RING
-    sub_rows = rows // SUBS
+    shared = rows // 2
+    sub_rows = shared // SUBS
     hops = (RING - 1) * SUBS * 2
     hbm = pl.BlockSpec(memory_space=pl.ANY)
     vmem = pl.BlockSpec(memory_space=pltpu.VMEM)
@@ -417,16 +543,24 @@
             pltpu.VMEM((RING - 1, SUBS, 2, sub_rows, HALF), BF16),
             pltpu.VMEM((RING - 1, SUBS, 2, sub_rows, HALF), BF16),
             pltpu.VMEM((rows, 2 * HALF), BF16),
+            pltpu.VMEM((heads, shared, FW), BF16),
+            pltpu.VMEM((heads, shared, FW), BF16),
+            pltpu.VMEM((RING, width, HALF), BF16),
+            pltpu.VMEM((heads, pulled, FW), BF16),
+            pltpu.VMEM((SUBS, 2, sub_rows, HALF), BF16),
+            pltpu.VMEM((SUBS, 2, sub_rows, HALF), BF16),
             pltpu.SemaphoreType.DMA((8,)),
             pltpu.SemaphoreType.DMA((2 * RING,)),
-            pltpu.SemaphoreType.DMA((SUBS + 1,)),
+            pltpu.SemaphoreType.DMA((2 * SUBS + 1,)),
             pltpu.SemaphoreType.DMA((COPIES,)),
             pltpu.SemaphoreType.DMA((COPIES,)),
             pltpu.SemaphoreType.DMA((hops,)),
             pltpu.SemaphoreType.DMA((hops,)),
+            pltpu.SemaphoreType.DMA((2 * SUBS,)),
+            pltpu.SemaphoreType.DMA((2 * SUBS,)),
         ],
         compiler_params=pltpu.CompilerParams(
-            collective_id=0, has_side_effects=True, vmem_limit_bytes=60 * MIB
+            collective_id=0, has_side_effects=True, vmem_limit_bytes=63 * MIB
         ),
         name="layer",
     )(query, keys, values, code_t, fast_weights, out_weight)

time: 137 us -> 119 us (0.87)
  Pallas kernels: 136 us -> 117 us
    pallas_call x1, Pallas kernels: 131 us -> 112 us  [layer(): pl.pallas_call(layer_kernel, out_shape=(jax.ShapeDtypeStruct((rows, 2 * H...]
where the time goes in v3:
time: 119 us; the launch traced here: 118 us
  Pallas kernels  117 us (98%)
    pallas_call x1, Pallas kernels, layer(): pl.pallas_call(layer_kernel, out_shape=(jax.ShapeDtypeStruct((rows, 2 * H...  112 us
    pallas_call x1, Pallas kernels, finish(): pl.pallas_call(finish_kernel, grid=(steps,), out_shape=(jax.ShapeDtypeStr...  5.51 us

profile of v3, /device:TPU:1, one launch (start us, length us, event | category | flops | bytes accessed | tf_op | source)
XLA Modules:
  0.0 117.7 jit_solution(1695962621226967931)
XLA Ops:
  0.6 111.6 %layer.1 = (bf16[1024,1024]{1,0:T(8,128)(2,1)}, bf16[2,1536,512]{2,1,0:T(8,128)(2,1)}) custom-call(bf16[1024,1024]{1,0:T(8,128)(2,1)} %q_hbm.1, bf16[1024,1024]{1,0:T(8,128)(2,1)} %k_hbm.1, bf16[1024,1024]{1,0:T(8,128)(2,1)} %v_hbm.1, s32[2,1024]{1,0:T(2,128)} %bitcast.1, bf16[2,3,512,512]{3,2,1,0:T(8,128)(2,1)} %fw_hbm.1, bf16[1024,4096]{1,0:T(8,128)(2,1)} %w_hbm.1), custom_call_target="tpu_custom_call" | custom-call | tf_op jit(solution)/shard_map/layer/pallas_call | solution.py:511
  112.2 5.5 %finish.1 = (bf16[1024,1024]{1,0:T(8,128)(2,1)}, bf16[2,3,512,512]{3,2,1,0:T(8,128)(2,1)}) custom-call(bf16[1024,1024]{1,0:T(8,128)(2,1)} %get-tuple-element.4.out_ref, bf16[2,1536,512]{2,1,0:T(8,128)(2,1)} %get-tuple-element.5.turned_ref), custom_call_target="tpu_custom_call" | custom-call | tf_op jit(solution)/shard_map/finish/pallas_call | solution.py:581

commit v4 on v2

v4 whole, which is shorter than its diff:
```python
import math

import jax
import jax.numpy as jnp
from jax import lax
from jax.experimental import pallas as pl
from jax.experimental.pallas import tpu as pltpu
from jax.sharding import PartitionSpec as P

FW = 512
HEAD_DIM = 128
WINDOW = 256
BASE_RATE = 0.05
BLOCK = 256
F32 = jnp.float32
BF16 = jnp.bfloat16
MESH = pl.DeviceIdType.MESH
MIB = 1024 * 1024


def dot(left, right, left_dim=1, right_dim=0):
    return lax.dot_general(
        left, right, (((left_dim,), (right_dim,)), ((), ())), preferred_element_type=F32
    )


def sigmoid(x):
    return 0.5 * jnp.tanh(0.5 * x) + 0.5


RING = 4
SHARED = 384
SUBS, SUB_ROWS = 4, 160
PAIR_SUBS, PAIR_ROWS = 2, 192
HALF = 512
COPIES = 96


def layer_kernel(
    q_hbm, k_hbm, v_hbm, code_ref, fw_hbm, w_hbm,
    out_hbm, new_hbm,
    q_buf, k_buf, v_buf, fw_buf, base_buf, d_buf, gated_buf, pushed_buf,
    grads, grad_in, in_u, sum_u, in_v,
    new_buf, rate_out, rate_in, att_buf, w_buf, merged, ring_out, ring_in, out_buf,
    q_pair, att_pair, w_pair, new_pair, pair_out, pair_in,
    load_sem, w_sem, store_sem, send_sem, recv_sem, ring_send, ring_recv, pair_send, pair_recv,
):
    ctx = lax.axis_index("ctx")
    me = lax.axis_index("head")
    core = lax.rem(ctx, 2)
    chip = lax.div(ctx, 2)
    y = lax.rem(chip, RING)
    x = lax.div(chip, RING)
    contexts = lax.axis_size("ctx")
    groups = lax.axis_size("head")
    rows = k_hbm.shape[0]
    tokens_all = rows * contexts
    blocks = rows // BLOCK
    part = in_u.shape[2]
    piece = in_v.shape[2]
    half = grads.shape[2]
    heads = fw_buf.shape[0]
    alone = rows - SHARED

    def at(xx, yy, cc):
        return (xx * RING + yy) * 2 + cc

    def ring_to(index):
        return lax.rem(index, RING)

    u = x + core * (y - x)
    v = y + core * (x - y)

    def at_uv(uu, vv):
        return at(uu + core * (vv - uu), vv + core * (uu - vv), core)

    partner = at(x, y, 1 - core)
    follower = lax.rem(ctx + 1, contexts)
    leader = lax.rem(ctx + contexts - 1, contexts)
    distances = range(1, RING)
    x_peer = [None] + [at(ring_to(x + d), y, core) for d in distances]
    y_peer = [None] + [at(x, ring_to(y + d), core) for d in distances]
    u_peer = [None] + [at_uv(ring_to(u + d), v) for d in distances]
    v_peer = [None] + [at_uv(u, ring_to(v + d)) for d in distances]
    opposite = lax.rem(me + 2, groups)
    ring_peer = (lax.rem(me + 1, groups), lax.rem(me + groups - 1, groups))

    def load(src, dst, index):
        return pltpu.make_async_copy(src, dst, load_sem.at[index])

    loads = {}
    for h in range(heads):
        lanes = pl.ds(h * FW, FW)
        loads["w", h] = load(fw_hbm.at[h], fw_buf.at[h], 4 * h)
        loads["k", h] = load(k_hbm.at[:, lanes], k_buf.at[h, pl.ds(WINDOW, rows)], 4 * h + 1)
        loads["v", h] = load(v_hbm.at[:, lanes], v_buf.at[h, pl.ds(WINDOW, rows)], 4 * h + 2)
        loads["q", h] = load(q_hbm.at[:, lanes], q_buf.at[h], 4 * h + 3)

    def w_columns(step, way):
        dest = lax.rem(me + groups - 1 - step, groups) if way == 0 else lax.rem(me + 1 + step, groups)
        return pl.ds(pl.multiple_of(dest * (2 * HALF) + way * HALF, HALF), HALF)

    w_loads = {}
    for step in range(RING):
        for way in range(2):
            index = 2 * step + way
            w_loads[step, way] = pltpu.make_async_copy(
                w_hbm.at[:, w_columns(step, way)], w_buf.at[index], w_sem.at[index]
            )
    for h in range(heads):
        for name in ("k", "v", "w"):
            loads[name, h].start()
    for h in range(heads):
        loads["q", h].start()

    barrier = pltpu.get_barrier_semaphore()
    ctx_peers = [follower, leader] + x_peer[1:] + y_peer[1:]
    for peer in ctx_peers:
        pl.semaphore_signal(barrier, inc=1, device_id={"ctx": peer}, device_id_type=MESH)
    head_peers = ring_peer + (opposite,)
    for peer in head_peers:
        pl.semaphore_signal(barrier, inc=1, device_id={"head": peer}, device_id_type=MESH)

    sent = []

    def send(src, dst, peer, axis="ctx"):
        index = len(sent)
        assert index < COPIES
        copy = pltpu.make_async_remote_copy(
            src_ref=src, dst_ref=dst, send_sem=send_sem.at[index], recv_sem=recv_sem.at[index],
            device_id={axis: peer}, device_id_type=MESH,
        )
        copy.start()
        sent.append(copy)
        return copy

    def aligned(start, size):
        return pl.ds(pl.multiple_of(start, 16), size)

    def train(head, begin, end):
        def tokens(t, carry):
            start = pl.multiple_of(t * BLOCK, BLOCK)
            k_rows = k_buf[head, pl.ds(start + WINDOW, BLOCK)]
            v_rows = v_buf[head, pl.ds(start + WINDOW, BLOCK)].astype(F32)
            code_row = code_ref[head : head + 1, pl.ds(start, BLOCK)].astype(F32) * 2.0 ** (-14)
            column = jnp.transpose(jnp.broadcast_to(code_row, (8, BLOCK)))[:, 0:1]
            pushed = (column * v_rows).astype(BF16)
            gate_in = dot(k_rows, fw_buf[head, 0])
            up_in = dot(k_rows, fw_buf[head, 1])
            back = dot(pushed, fw_buf[head, 2], 1, 1)
            s = sigmoid(gate_in)
            gs = gate_in * s
            here = pl.ds(start, BLOCK)
            pushed_buf[here] = pushed
            gated_buf[here] = (gs * up_in).astype(BF16)
            d_buf[here, 0:FW] = (back * up_in * (s * (1.0 + gate_in * (1.0 - s)))).astype(BF16)
            d_buf[here, FW : 2 * FW] = (back * gs).astype(BF16)
            return carry

        lax.fori_loop(begin, end, tokens, 0)

    def pulls(head):
        k_own = k_buf.at[head, pl.ds(WINDOW, rows)]
        per_half = half // BLOCK
        for i in range(3 * FW // BLOCK):
            if i < 2 * FW // BLOCK:
                value = dot(d_buf[:, i * BLOCK : (i + 1) * BLOCK], k_own[...], 0, 0)
            else:
                first = i * BLOCK - 2 * FW
                value = dot(pushed_buf[:, first : first + BLOCK], gated_buf[...], 0, 0)
            where = pl.ds(i % per_half * BLOCK, BLOCK)
            grads[head, i // per_half, where] = value.astype(BF16)

    def send_core(h):
        return send(grads.at[h, 1 - core], grad_in.at[h], partner)

    def send_u(h):
        grads[h, core] = (grads[h, core].astype(F32) + grad_in[h].astype(F32)).astype(BF16)
        return [
            send(grads.at[h, core, aligned(ring_to(u + d) * part, part)], in_u.at[h, d - 1], u_peer[d])
            for d in distances
        ]

    def total(own, others):
        value = own.astype(F32)
        for i in range(RING - 1):
            value = value + others[i].astype(F32)
        return value

    def send_v(h):
        sum_u[h] = total(grads[h, core, aligned(u * part, part)], in_u.at[h]).astype(BF16)
        return [
            send(sum_u.at[h, aligned(ring_to(v + d) * piece, piece)], in_v.at[h, d - 1], v_peer[d])
            for d in distances
        ]

    mine = aligned(core * half + u * part + v * piece, piece)

    def renorm(h):
        base = base_buf[h, aligned(u * part + v * piece, piece)].astype(F32)
        pull = total(sum_u[h, aligned(v * piece, piece)], in_v.at[h])
        step_size = BASE_RATE / (math.sqrt(tokens_all) * (rate_out[3, h : h + 1, 0:1] / tokens_all))
        updated = base + step_size * pull
        old_norm = jnp.sqrt(jnp.sum(base * base, axis=1, keepdims=True) + 1e-06)
        new_norm = jnp.sqrt(jnp.sum(updated * updated, axis=1, keepdims=True) + 1e-06)
        new_buf[h, mine] = (updated * (old_norm / new_norm)).astype(BF16)

    def spread_v(buf, h):
        return [send(buf.at[h, mine], buf.at[h, mine], v_peer[d]) for d in distances]

    def spread_u(buf, h):
        whole = buf.at[h, aligned(core * half + u * part, part)]
        return [send(whole, whole, u_peer[d]) for d in distances]

    def spread_core(buf, h):
        whole = buf.at[h, aligned(core * half, half)]
        return send(whole, whole, partner)

    def forward_own(h):
        whole = new_buf.at[h, aligned(core * half + u * part, part)]
        return [send(whole, whole, partner)]

    def forward(copies, h):
        out = []
        for d in (1, 3, 2):
            copies[d - 1].wait_recv()
            whole = new_buf.at[h, aligned(core * half + ring_to(u + RING - d) * part, part)]
            out.append(send(whole, whole, partner))
        return out

    def received(copies):
        for copy in copies:
            copy.wait_recv()

    row_id = lax.broadcasted_iota(jnp.int32, (BLOCK, BLOCK), 0)
    col_id = lax.broadcasted_iota(jnp.int32, (BLOCK, BLOCK), 1)
    scale = math.log2(math.e) / math.sqrt(HEAD_DIM)

    def attend(unit, carry):
        head = lax.rem(unit, heads)
        block = blocks - 1 - lax.div(unit, heads)
        start = pl.multiple_of(block * BLOCK, BLOCK)
        unseen = jnp.where((ctx == 0) & (block == 0), -1e30, 0.0).astype(F32)
        causal = col_id <= row_id
        for j in range(FW // HEAD_DIM):
            cols = pl.ds(j * HEAD_DIM, HEAD_DIM)
            q_rows = q_buf[head, pl.ds(start, BLOCK), cols]
            scores = dot(q_rows, k_buf[head, pl.ds(start, 2 * BLOCK), cols], 1, 1)
            live = jnp.where(causal, scores[:, BLOCK:], scores[:, :BLOCK] + unseen)
            top = jnp.max(live, axis=1, keepdims=True)
            exps = jnp.exp2((live - top) * scale)
            old = jnp.where(causal, 0.0, exps).astype(BF16)
            new = jnp.where(causal, exps, 0.0).astype(BF16)
            ones = jnp.ones((BLOCK, HEAD_DIM), BF16)
            v_old = jnp.concatenate([v_buf[head, pl.ds(start, BLOCK), cols], ones], 1)
            v_new = jnp.concatenate([v_buf[head, pl.ds(start + BLOCK, BLOCK), cols], ones], 1)
            both = dot(old, v_old) + dot(new, v_new)
            att_buf[head, pl.ds(start, BLOCK), cols] = (
                both[:, :HEAD_DIM] / both[:, HEAD_DIM:]
            ).astype(BF16)
        return carry

    def attention(begin, end):
        lax.fori_loop(begin, end, attend, 0)

    rate = code_ref[...].astype(F32) * 2.0 ** (-14)
    rate_out[0] = jnp.broadcast_to(jnp.sum(rate, axis=1, keepdims=True), rate_out.shape[1:])
    slice_rows = w_buf.shape[1] // contexts
    part_rows = slice_rows * RING
    w_own_a = aligned(((core * RING + x) * RING + y) * slice_rows, slice_rows)
    w_own_b = aligned(((core * RING + y) * RING + x) * slice_rows, slice_rows)
    one, two = pl.ds(0, 2), pl.ds(2, 2)

    pl.semaphore_wait(barrier, len(ctx_peers) + len(head_peers))
    edge, rim = pl.ds(rows - WINDOW, WINDOW), pl.ds(0, WINDOW)
    rims = []
    for h in range(heads):
        lanes = pl.ds(h * FW, FW)
        rims.append(send(k_hbm.at[edge, lanes], k_buf.at[h, rim], follower))
        rims.append(send(v_hbm.at[edge, lanes], v_buf.at[h, rim], follower))
    w_z = []
    for slot in range(RING):
        where = (w_own_a, w_own_b)[slot // 2]
        src = w_hbm.at[where, w_columns(slot // 2, slot % 2)]
        w_z.append(send(src, w_pair.at[slot, where], opposite, "head"))
    pair_q = []
    for h in range(heads):
        src = q_hbm.at[pl.ds(alone, SHARED), pl.ds(h * FW, FW)]
        pair_q.append(send(src, q_pair.at[h], opposite, "head"))
    core_rate = send(rate_out.at[0], rate_in.at[0], partner)
    for name in ("k", "v", "w"):
        loads[name, 0].wait()
    train(0, 0, blocks)
    for copy in w_loads.values():
        copy.start()
    pulls(0)
    core_0 = send_core(0)
    for name in ("k", "v", "w"):
        loads[name, 1].wait()
    train(1, 0, blocks)
    core_rate.wait_recv()
    rate_out[1] = rate_out[0] + rate_in[0]
    core_0.wait_recv()
    u_0 = send_u(0) + [send(rate_out.at[1], rate_in.at[d], x_peer[d]) for d in distances]
    pulls(1)
    core_1 = send_core(1)
    for h in range(heads):
        for i in range(half // BLOCK):
            block = core * (half // BLOCK) + i
            cols = pl.ds(pl.multiple_of(lax.rem(block, 2) * BLOCK, BLOCK), BLOCK)
            base_buf[h, i * BLOCK : (i + 1) * BLOCK] = jnp.transpose(fw_buf[h, lax.div(block, 2), :, cols])
    for h in range(heads):
        loads["q", h].wait()
    attention(0, 2)
    core_1.wait_recv()
    u_1 = send_u(1)
    attention(2, 4)
    pair_att = send(att_buf.at[:, pl.ds(alone, SHARED)], att_pair, opposite, "head")
    received(u_0)
    rate_out[2] = rate_out[1] + rate_in[1] + rate_in[2] + rate_in[3]
    v_0 = send_v(0) + [send(rate_out.at[2], rate_in.at[RING - 1 + d], y_peer[d]) for d in distances]
    attention(4, 5)
    received(u_1)
    v_1 = send_v(1)
    received(v_0)
    rate_out[3] = rate_out[2] + rate_in[4] + rate_in[5] + rate_in[6]
    renorm(0)
    back_0 = spread_v(new_buf, 0)
    new_z = [send(new_buf.at[0, mine], new_pair.at[0, mine], opposite, "head")]
    attention(5, 6)
    received(back_0)
    whole_0 = spread_u(new_buf, 0)
    across_0 = forward_own(0)
    received(v_1)
    renorm(1)
    back_1 = spread_v(new_buf, 1)
    new_z.append(send(new_buf.at[1, mine], new_pair.at[1, mine], opposite, "head"))
    received(rims)
    attention(6, 8)
    received(back_1)
    whole_1 = spread_u(new_buf, 1)
    across_1 = forward_own(1)
    for copy in w_loads.values():
        copy.wait()
    across_0 += forward(whole_0, 0)

    def hop(step, sub, way):
        index = (step * SUBS + sub) * 2 + way
        return pltpu.make_async_remote_copy(
            src_ref=ring_out.at[step, sub, way], dst_ref=ring_in.at[step, sub, way],
            send_sem=ring_send.at[index], recv_sem=ring_recv.at[index],
            device_id={"head": ring_peer[way]}, device_id_type=MESH,
        )

    def pair_hop(sub, way):
        index = sub * 2 + way
        return pltpu.make_async_remote_copy(
            src_ref=pair_out.at[sub, way], dst_ref=pair_in.at[sub, way],
            send_sem=pair_send.at[index], recv_sem=pair_recv.at[index],
            device_id={"head": ring_peer[way]}, device_id_type=MESH,
        )

    def chunk(sub):
        return aligned(sub * SUB_ROWS, SUB_ROWS)

    def pair_chunk(sub):
        return aligned(alone + sub * PAIR_ROWS, PAIR_ROWS)

    def partial(step, sub, way):
        return dot(merged[chunk(sub)], w_buf[2 * step + way])

    merged_pair = d_buf

    def partial_pair(step, sub, way, slot):
        theirs = merged_pair[aligned(sub * PAIR_ROWS, PAIR_ROWS), 0 : heads * FW]
        return dot(merged[pair_chunk(sub)], w_buf[2 * step + way]) + dot(theirs, w_pair[slot])

    def apply(q_rows, weights, attended, h):
        gate_in = dot(q_rows, weights[h, 0:FW], 1, 1)
        up_in = dot(q_rows, weights[h, FW : 2 * FW], 1, 1)
        gated = (gate_in * sigmoid(gate_in) * up_in).astype(BF16)
        value = dot(gated, weights[h, 2 * FW : 3 * FW], 1, 1)
        norm = lax.rsqrt(jnp.mean(value * value, axis=1, keepdims=True) + 1e-06)
        return (attended.astype(F32) + value * norm).astype(BF16)

    def apply_own(here, h):
        merged[here, h * FW : (h + 1) * FW] = apply(q_buf[h, here], new_buf, att_buf[h, here], h)

    double = 2 * SUB_ROWS

    def opening_0(pair, carry):
        apply_own(aligned(pair * double, double), 0)
        return carry

    def opening_1(pair, carry):
        apply_own(aligned(pair * double, double), 1)
        for i in range(2):
            sub = 2 * pair + i
            for way in range(2):
                ring_out[0, sub, way] = partial(0, sub, way).astype(BF16)
                hop(0, sub, way).start()
        return carry

    def store_out(here, index):
        return pltpu.make_async_copy(out_buf.at[here], out_hbm.at[here], store_sem.at[index])

    def round_ring(step, begin=0, end=SUBS):
        def middle(sub, carry):
            for way in range(2):
                own = partial(step, sub, way)
                hop(step - 1, sub, way).wait_recv()
                value = (own + ring_in[step - 1, sub, way].astype(F32)).astype(BF16)
                if step < RING - 1:
                    ring_out[step, sub, way] = value
                    hop(step, sub, way).start()
                else:
                    out_buf[chunk(sub), way * HALF : (way + 1) * HALF] = value
            if step == RING - 1:
                store_out(chunk(sub), sub).start()
            return carry

        lax.fori_loop(begin, end, middle, 0)

    received(across_0)
    lax.fori_loop(0, SUBS // 2, opening_0, 0)
    across_1 += forward(whole_1, 1)
    received(w_z)
    w_1 = []
    for d in distances:
        w_1.append(send(w_pair.at[one, w_own_a], w_pair.at[one, w_own_a], y_peer[d]))
        w_1.append(send(w_pair.at[two, w_own_b], w_pair.at[two, w_own_b], x_peer[d]))
    received(across_1)
    lax.fori_loop(0, SUBS // 2, opening_1, 0)

    received(new_z)
    pair_v = spread_v(new_pair, 0) + spread_v(new_pair, 1)
    for h in range(heads):
        apply_own(pl.ds(alone, SHARED), h)
    received(w_1)
    w_2 = []
    for d in distances:
        w_x = w_pair.at[one, aligned((core * RING + x) * part_rows, part_rows)]
        w_y = w_pair.at[two, aligned((core * RING + y) * part_rows, part_rows)]
        w_2.append(send(w_x, w_x, x_peer[d]))
        w_2.append(send(w_y, w_y, y_peer[d]))
    for h in range(heads):
        for m in range(3):
            fw_buf[h, m] = jnp.transpose(new_buf[h, m * FW : (m + 1) * FW])
    store_new = pltpu.make_async_copy(fw_buf, new_hbm, store_sem.at[SUBS + PAIR_SUBS])
    store_new.start()
    round_ring(1)
    received(pair_v)
    pair_u = spread_u(new_pair, 0) + spread_u(new_pair, 1)
    round_ring(2, 0, SUBS // 2)
    received(w_2)
    w_half = w_pair.at[:, aligned(core * RING * part_rows, RING * part_rows)]
    w_across = send(w_half, w_half, partner)
    round_ring(2, SUBS // 2, SUBS)
    received(pair_u)
    pair_across = [spread_core(new_pair, 0), spread_core(new_pair, 1)]
    received(pair_q)
    pair_att.wait_recv()
    received(pair_across)
    w_across.wait_recv()

    for h in range(heads):
        merged_pair[0:SHARED, h * FW : (h + 1) * FW] = apply(q_pair[h], new_pair, att_pair[h], h)

    def opening_pair(sub, carry):
        for way in range(2):
            pair_out[sub, way] = partial_pair(2, sub, way, way).astype(BF16)
            pair_hop(sub, way).start()
        return carry

    lax.fori_loop(0, PAIR_SUBS, opening_pair, 0)
    round_ring(3)

    def closing_pair(sub, carry):
        here = pair_chunk(sub)
        for way in range(2):
            own = partial_pair(3, sub, way, 2 + way)
            pair_hop(sub, way).wait_recv()
            out_buf[here, way * HALF : (way + 1) * HALF] = (
                own + pair_in[sub, way].astype(F32)
            ).astype(BF16)
        store_out(here, SUBS + sub).start()
        return carry

    lax.fori_loop(0, PAIR_SUBS, closing_pair, 0)

    for copy in sent:
        copy.wait_send()

    def drain(sub, carry):
        for way in range(2):
            for step in range(RING - 1):
                hop(step, sub, way).wait_send()
        return carry

    lax.fori_loop(0, SUBS, drain, 0)
    for sub in range(PAIR_SUBS):
        for way in range(2):
            pair_hop(sub, way).wait_send()
    for sub in range(SUBS):
        store_out(chunk(sub), sub).wait()
    for sub in range(PAIR_SUBS):
        store_out(pair_chunk(sub), SUBS + sub).wait()
    store_new.wait()


def layer(query, keys, values, code_t, fast_weights, out_weight):
    rows, width = query.shape
    heads = width // FW
    pulled = 3 * FW
    half = pulled // 2
    part = half // RING
    piece = part // RING
    hops = (RING - 1) * SUBS * 2
    hbm = pl.BlockSpec(memory_space=pl.ANY)
    vmem = pl.BlockSpec(memory_space=pltpu.VMEM)
    return pl.pallas_call(
        layer_kernel,
        out_shape=(
            jax.ShapeDtypeStruct((rows, 2 * HALF), BF16),
            jax.ShapeDtypeStruct(fast_weights.shape, BF16),
        ),
        in_specs=[hbm, hbm, hbm, vmem, hbm, hbm],
        out_specs=(hbm, hbm),
        scratch_shapes=[
            pltpu.VMEM((heads, rows, FW), BF16),
            pltpu.VMEM((heads, rows + WINDOW, FW), BF16),
            pltpu.VMEM((heads, rows + WINDOW, FW), BF16),
            pltpu.VMEM((heads, 3, FW, FW), BF16),
            pltpu.VMEM((heads, half, FW), BF16),
            pltpu.VMEM((rows, 2 * FW), BF16),
            pltpu.VMEM((rows, FW), BF16),
            pltpu.VMEM((rows, FW), BF16),
            pltpu.VMEM((heads, 2, half, FW), BF16),
            pltpu.VMEM((heads, half, FW), BF16),
            pltpu.VMEM((heads, RING - 1, part, FW), BF16),
            pltpu.VMEM((heads, part, FW), BF16),
            pltpu.VMEM((heads, RING - 1, piece, FW), BF16),
            pltpu.VMEM((heads, pulled, FW), BF16),
            pltpu.VMEM((4, heads, 128), F32),
            pltpu.VMEM((7, heads, 128), F32),
            pltpu.VMEM((heads, rows, FW), BF16),
            pltpu.VMEM((2 * RING, width, HALF), BF16),
            pltpu.VMEM((rows, width), BF16),
            pltpu.VMEM((RING - 1, SUBS, 2, SUB_ROWS, HALF), BF16),
            pltpu.VMEM((RING - 1, SUBS, 2, SUB_ROWS, HALF), BF16),
            pltpu.VMEM((rows, 2 * HALF), BF16),
            pltpu.VMEM((heads, SHARED, FW), BF16),
            pltpu.VMEM((heads, SHARED, FW), BF16),
            pltpu.VMEM((RING, width, HALF), BF16),
            pltpu.VMEM((heads, pulled, FW), BF16),
            pltpu.VMEM((PAIR_SUBS, 2, PAIR_ROWS, HALF), BF16),
            pltpu.VMEM((PAIR_SUBS, 2, PAIR_ROWS, HALF), BF16),
            pltpu.SemaphoreType.DMA((8,)),
            pltpu.SemaphoreType.DMA((2 * RING,)),
            pltpu.SemaphoreType.DMA((SUBS + PAIR_SUBS + 1,)),
            pltpu.SemaphoreType.DMA((COPIES,)),
            pltpu.SemaphoreType.DMA((COPIES,)),
            pltpu.SemaphoreType.DMA((hops,)),
            pltpu.SemaphoreType.DMA((hops,)),
            pltpu.SemaphoreType.DMA((2 * PAIR_SUBS,)),
            pltpu.SemaphoreType.DMA((2 * PAIR_SUBS,)),
        ],
        compiler_params=pltpu.CompilerParams(
            collective_id=0, has_side_effects=True, vmem_limit_bytes=63 * MIB
        ),
        name="layer",
    )(query, keys, values, code_t, fast_weights, out_weight)


FINISH_STEPS = 4


def finish_kernel(out_hbm, new_hbm, final_hbm, final_new_hbm, out_buf, new_buf, in_sem, out_sem):
    copies = []
    for source, target, buf in ((new_hbm, final_new_hbm, new_buf), (out_hbm, final_hbm, out_buf)):
        size = source.shape[0] // FINISH_STEPS
        for i in range(FINISH_STEPS):
            index = len(copies)
            here = pl.ds(i * size, size)
            take = pltpu.make_async_copy(source.at[here], buf.at[here], in_sem.at[index])
            take.start()
            copies.append((take, pltpu.make_async_copy(buf.at[here], target.at[here], out_sem.at[index])))
    for take, put in copies:
        take.wait()
        put.start()
    for take, put in copies:
        put.wait()


def finish(out, new_weights):
    heads, mats, inner, width = new_weights.shape
    flat = new_weights.reshape(heads * mats * inner, width)
    hbm = pl.BlockSpec(memory_space=pl.ANY)
    out, flat = pl.pallas_call(
        finish_kernel,
        out_shape=(jax.ShapeDtypeStruct(out.shape, BF16), jax.ShapeDtypeStruct(flat.shape, BF16)),
        in_specs=[hbm, hbm],
        out_specs=(hbm, hbm),
        scratch_shapes=[
            pltpu.VMEM(out.shape, BF16),
            pltpu.VMEM(flat.shape, BF16),
            pltpu.SemaphoreType.DMA((2 * FINISH_STEPS,)),
            pltpu.SemaphoreType.DMA((2 * FINISH_STEPS,)),
        ],
        name="finish",
    )(out, flat)
    return out, flat.reshape(new_weights.shape)


def shards(query, keys, values, lr_code, fast_weights, out_weight):
    out, new_weights = layer(query, keys, values, lr_code.T, fast_weights, out_weight)
    return finish(out, new_weights)


def solution(mesh):
    placed = (
        P("ctx", "head"),
        P("ctx", "head"),
        P("ctx", "head"),
        P("ctx", "head"),
        P("head", None, None, None),
        P("head", None),
    )
    return jax.shard_map(
        shards,
        mesh=mesh,
        in_specs=placed,
        out_specs=(P("ctx", "head"), P("head", None, None, None)),
        check_vma=False,
    )
```

time: 137 us -> 117 us (0.85)
  Pallas kernels: 136 us -> 116 us
    pallas_call x1, Pallas kernels: 131 us -> 111 us  [layer(): pl.pallas_call(layer_kernel, out_shape=(jax.ShapeDtypeStruct((rows, 2 * H...]
where the time goes in v4:
time: 117 us; the launch traced here: 116 us
  Pallas kernels  116 us (99%)
    pallas_call x1, Pallas kernels, layer(): pl.pallas_call(layer_kernel, out_shape=(jax.ShapeDtypeStruct((rows, 2 * H...  111 us
    pallas_call x1, Pallas kernels, finish(): pl.pallas_call(finish_kernel, out_shape=(jax.ShapeDtypeStruct(out.shape,...  4.46 us

profile of v4, /device:TPU:1, one launch (start us, length us, event | category | flops | bytes accessed | tf_op | source)
XLA Modules:
  0.0 116.4 jit_solution(12049258717535886768)
XLA Ops:
  0.6 111.2 %layer.1 = (bf16[1024,1024]{1,0:T(8,128)(2,1)}, bf16[2,3,512,512]{3,2,1,0:T(8,128)(2,1)}) custom-call(bf16[1024,1024]{1,0:T(8,128)(2,1)} %q_hbm.1, bf16[1024,1024]{1,0:T(8,128)(2,1)} %k_hbm.1, bf16[1024,1024]{1,0:T(8,128)(2,1)} %v_hbm.1, s32[2,1024]{1,0:T(2,128)} %bitcast.4, bf16[2,3,512,512]{3,2,1,0:T(8,128)(2,1)} %fw_hbm.1, bf16[1024,4096]{1,0:T(8,128)(2,1)} %w_hbm.1), custom_call_target="tpu_custom_call" | custom-call | tf_op jit(solution)/shard_map/layer/pallas_call | solution.py:521
  111.8 4.5 %finish.1 = (bf16[1024,1024]{1,0:T(8,128)(2,1)}, bf16[3072,512]{1,0:T(8,128)(2,1)}) custom-call(bf16[1024,1024]{1,0:T(8,128)(2,1)} %get-tuple-element.6.out_hbm, bf16[3072,512]{1,0:T(8,128)(2,1)} %bitcast.3), custom_call_target="tpu_custom_call" | custom-call | tf_op jit(solution)/shard_map/finish/pallas_call | solution.py:599

commit v5 on v4

--- a/solution.py
+++ b/solution.py
@@ -29,9 +29,9 @@
 
 
 RING = 4
-SHARED = 384
-SUBS, SUB_ROWS = 4, 160
-PAIR_SUBS, PAIR_ROWS = 2, 192
+SHARED = 448
+SUBS, SUB_ROWS = 4, 144
+PAIR_SUBS, PAIR_ROWS = 2, 224
 HALF = 512
 COPIES = 96
 
@@ -277,7 +277,8 @@
     for h in range(heads):
         lanes = pl.ds(h * FW, FW)
         rims.append(send(k_hbm.at[edge, lanes], k_buf.at[h, rim], follower))
-        rims.append(send(v_hbm.at[edge, lanes], v_buf.at[h, rim], follower))
+        if h == 0:
+            rims.append(send(v_hbm.at[edge, lanes], v_buf.at[h, rim], follower))
     w_z = []
     for slot in range(RING):
         where = (w_own_a, w_own_b)[slot // 2]
@@ -322,6 +323,7 @@
     attention(4, 5)
     received(u_1)
     v_1 = send_v(1)
+    rims.append(send(v_buf.at[1, pl.ds(rows, WINDOW)], v_buf.at[1, rim], follower))
     received(v_0)
     rate_out[3] = rate_out[2] + rate_in[4] + rate_in[5] + rate_in[6]
     renorm(0)
@@ -335,11 +337,11 @@
     renorm(1)
     back_1 = spread_v(new_buf, 1)
     new_z.append(send(new_buf.at[1, mine], new_pair.at[1, mine], opposite, "head"))
-    received(rims)
-    attention(6, 8)
     received(back_1)
     whole_1 = spread_u(new_buf, 1)
     across_1 = forward_own(1)
+    received(rims)
+    attention(6, 8)
     for copy in w_loads.values():
         copy.wait()
     across_0 += forward(whole_0, 0)

time: 117 us -> 111 us (0.949)
  Pallas kernels: 116 us -> 110 us
    pallas_call x1, Pallas kernels: 111 us -> 106 us  [layer(): pl.pallas_call(layer_kernel, out_shape=(jax.ShapeDtypeStruct((rows, 2 * H...]
where the time goes in v5:
time: 111 us
  Pallas kernels  110 us (99%)
    pallas_call x1, Pallas kernels, layer(): pl.pallas_call(layer_kernel, out_shape=(jax.ShapeDtypeStruct((rows, 2 * H...  106 us
    pallas_call x1, Pallas kernels, finish(): pl.pallas_call(finish_kernel, out_shape=(jax.ShapeDtypeStruct(out.shape,...  4.46 us

profile of v5, /device:TPU:1, one launch (start us, length us, event | category | flops | bytes accessed | tf_op | source)
XLA Modules:
  0.0 111.1 jit_solution(9848273646592858968)
XLA Ops:
  0.6 105.9 %layer.1 = (bf16[1024,1024]{1,0:T(8,128)(2,1)}, bf16[2,3,512,512]{3,2,1,0:T(8,128)(2,1)}) custom-call(bf16[1024,1024]{1,0:T(8,128)(2,1)} %q_hbm.1, bf16[1024,1024]{1,0:T(8,128)(2,1)} %k_hbm.1, bf16[1024,1024]{1,0:T(8,128)(2,1)} %v_hbm.1, s32[2,1024]{1,0:T(2,128)} %bitcast.4, bf16[2,3,512,512]{3,2,1,0:T(8,128)(2,1)} %fw_hbm.1, bf16[1024,4096]{1,0:T(8,128)(2,1)} %w_hbm.1), custom_call_target="tpu_custom_call" | custom-call | tf_op jit(solution)/shard_map/layer/pallas_call | solution.py:523
  106.5 4.5 %finish.1 = (bf16[1024,1024]{1,0:T(8,128)(2,1)}, bf16[3072,512]{1,0:T(8,128)(2,1)}) custom-call(bf16[1024,1024]{1,0:T(8,128)(2,1)} %get-tuple-element.6.out_hbm, bf16[3072,512]{1,0:T(8,128)(2,1)} %bitcast.3), custom_call_target="tpu_custom_call" | custom-call | tf_op jit(solution)/shard_map/finish/pallas_call | solution.py:601

commit v6 on v5

--- a/solution.py
+++ b/solution.py
@@ -330,13 +330,13 @@
     back_0 = spread_v(new_buf, 0)
     new_z = [send(new_buf.at[0, mine], new_pair.at[0, mine], opposite, "head")]
     attention(5, 6)
-    received(back_0)
-    whole_0 = spread_u(new_buf, 0)
-    across_0 = forward_own(0)
     received(v_1)
     renorm(1)
     back_1 = spread_v(new_buf, 1)
     new_z.append(send(new_buf.at[1, mine], new_pair.at[1, mine], opposite, "head"))
+    received(back_0)
+    whole_0 = spread_u(new_buf, 0)
+    across_0 = forward_own(0)
     received(back_1)
     whole_1 = spread_u(new_buf, 1)
     across_1 = forward_own(1)
@@ -394,13 +394,11 @@
         apply_own(aligned(pair * double, double), 0)
         return carry
 
-    def opening_1(pair, carry):
-        apply_own(aligned(pair * double, double), 1)
-        for i in range(2):
-            sub = 2 * pair + i
-            for way in range(2):
-                ring_out[0, sub, way] = partial(0, sub, way).astype(BF16)
-                hop(0, sub, way).start()
+    def opening_1(sub, carry):
+        apply_own(chunk(sub), 1)
+        for way in range(2):
+            ring_out[0, sub, way] = partial(0, sub, way).astype(BF16)
+            hop(0, sub, way).start()
         return carry
 
     def store_out(here, index):
@@ -432,7 +430,7 @@
         w_1.append(send(w_pair.at[one, w_own_a], w_pair.at[one, w_own_a], y_peer[d]))
         w_1.append(send(w_pair.at[two, w_own_b], w_pair.at[two, w_own_b], x_peer[d]))
     received(across_1)
-    lax.fori_loop(0, SUBS // 2, opening_1, 0)
+    lax.fori_loop(0, SUBS, opening_1, 0)
 
     received(new_z)
     pair_v = spread_v(new_pair, 0) + spread_v(new_pair, 1)
@@ -574,7 +572,7 @@
     )(query, keys, values, code_t, fast_weights, out_weight)
 
 
-FINISH_STEPS = 4
+FINISH_STEPS = 2
 
 
 def finish_kernel(out_hbm, new_hbm, final_hbm, final_new_hbm, out_buf, new_buf, in_sem, out_sem):

time: 111 us -> 111 us (level)
  no operation moved by 1% of the time
where the time goes in v6:
time: 111 us; the launch traced here: 110 us
  Pallas kernels  110 us (99%)
    pallas_call x1, Pallas kernels, layer(): pl.pallas_call(layer_kernel, out_shape=(jax.ShapeDtypeStruct((rows, 2 * H...  106 us
    pallas_call x1, Pallas kernels, finish(): pl.pallas_call(finish_kernel, out_shape=(jax.ShapeDtypeStruct(out.shape,...  3.91 us

profile of v6, /device:TPU:1, one launch (start us, length us, event | category | flops | bytes accessed | tf_op | source)
XLA Modules:
  0.0 110.4 jit_solution(5490723573180174949)
XLA Ops:
  0.6 105.7 %layer.1 = (bf16[1024,1024]{1,0:T(8,128)(2,1)}, bf16[2,3,512,512]{3,2,1,0:T(8,128)(2,1)}) custom-call(bf16[1024,1024]{1,0:T(8,128)(2,1)} %q_hbm.1, bf16[1024,1024]{1,0:T(8,128)(2,1)} %k_hbm.1, bf16[1024,1024]{1,0:T(8,128)(2,1)} %v_hbm.1, s32[2,1024]{1,0:T(2,128)} %bitcast.4, bf16[2,3,512,512]{3,2,1,0:T(8,128)(2,1)} %fw_hbm.1, bf16[1024,4096]{1,0:T(8,128)(2,1)} %w_hbm.1), custom_call_target="tpu_custom_call" | custom-call | tf_op jit(solution)/shard_map/layer/pallas_call | solution.py:521
  106.3 3.9 %finish.1 = (bf16[1024,1024]{1,0:T(8,128)(2,1)}, bf16[3072,512]{1,0:T(8,128)(2,1)}) custom-call(bf16[1024,1024]{1,0:T(8,128)(2,1)} %get-tuple-element.6.out_hbm, bf16[3072,512]{1,0:T(8,128)(2,1)} %bitcast.3), custom_call_target="tpu_custom_call" | custom-call | tf_op jit(solution)/shard_map/finish/pallas_call | solution.py:599
